TPU v7x, 768 devices: a whole 4x8x12 slice. The times are simulated.
768 devices in a mesh: blk: 192 (over z_hi, x, y, core), grp: 4 (over z_lo).
Axes of the slice: x: 4, y: 8, z: 12 (z_hi: 3, z_lo: 4; z = z_hi * 4 + z_lo), core: 2. Of those that a mesh axis runs over, the one named last changes fastest.
Arguments:
- image_embeds: bfloat16 [98304, 1152], P(('blk', 'grp')), may hold values from -6 to 6
- text_embeds: bfloat16 [98304, 1152], P(('blk', 'grp')), may hold values from -6 to 6
Outputs:
- image_embed_gradient: bfloat16 [98304, 1152], P(('blk', 'grp'))
- text_embed_gradient: bfloat16 [98304, 1152], P(('blk', 'grp'))
All inputs are finite; a program needn't handle non-finite values.
Results may differ from a plain program's by a relative error of at most 0.0059.
Values may be sent and summed in bfloat16 or wider, within the bound.
A program may use at most 64 MiB of HBM per device.

v0:
```python
import jax
import jax.numpy as jnp
from jax import lax
from jax.sharding import PartitionSpec as P

LOGIT_SCALE = 10.0
BIAS_LOGIT = -2.0
EPSILON = 1e-06


def shifted(value, axis, steps):
    count = lax.axis_size(axis)
    pairs = [(source, (source + steps) % count) for source in range(count)]
    return lax.ppermute(value, axis, pairs)


def normalize(values):
    wide = values.astype(jnp.float32)
    length = jnp.sqrt(jnp.sum(wide * wide, axis=-1, keepdims=True) + EPSILON)
    return (wide / length, length)


def undo_normalization(grad, unit, length):
    inner = jnp.sum(unit * grad, axis=-1, keepdims=True)
    return (grad - unit * inner) / length


def pair_weights(image_block, text_block, is_first):
    pair_logits = (
        LOGIT_SCALE
        * lax.dot_general(
            image_block, text_block, (((1,), (1,)), ((), ())), preferred_element_type=jnp.float32
        )
        + BIAS_LOGIT
    )
    count = pair_logits.shape[-1]
    diagonal_mask = jnp.eye(count, dtype=bool) & is_first
    weights = jnp.where(diagonal_mask, -jax.nn.sigmoid(-pair_logits), jax.nn.sigmoid(pair_logits))
    return weights.astype(jnp.bfloat16)


def text_terms(weights, image_block):
    return lax.dot_general(
        weights, image_block, (((0,), (0,)), ((), ())), preferred_element_type=jnp.float32
    )


def per_device(image_embeds, text_embeds):
    cycle_size = lax.axis_size(("blk", "grp"))
    window = min(20, cycle_size // 2)
    image_normalized, image_norm = normalize(image_embeds)
    text_normalized, text_norm = normalize(text_embeds)
    image_reduced = image_normalized.astype(jnp.bfloat16)
    text_low = text_normalized.astype(jnp.bfloat16)

    def advance(running, offset):
        text_block, image_block, text_total, image_total = running
        is_first = offset == 0
        weights = pair_weights(image_reduced, text_block, is_first)
        image_total = image_total + jnp.dot(weights, text_block, preferred_element_type=jnp.float32)
        passed = shifted(text_block, ("blk", "grp"), 1)
        own_weights = pair_weights(image_block, text_low, is_first)
        text_total = text_total + text_terms(own_weights, image_block)
        image_block = shifted(image_block, ("blk", "grp"), -1)
        return ((passed, image_block, text_total, image_total), weights)

    zeros = jnp.zeros(image_reduced.shape, jnp.float32)
    (text_block, image_block, text_total, image_total), stored = lax.scan(
        advance, (text_low, image_reduced, zeros, zeros), jnp.arange(window - 1, dtype=jnp.int32)
    )
    last_first = jnp.asarray(window - 1) == 0
    final_weights = pair_weights(image_reduced, text_block, last_first)
    image_total = image_total + jnp.dot(
        final_weights, text_block, preferred_element_type=jnp.float32
    )
    own_weights = pair_weights(image_block, text_low, last_first)
    text_total = text_total + text_terms(own_weights, image_block)
    image_embed_gradient = undo_normalization(
        LOGIT_SCALE * image_total, image_normalized, image_norm
    ).astype(jnp.bfloat16)
    text_embed_gradient = undo_normalization(
        LOGIT_SCALE * text_total, text_normalized, text_norm
    ).astype(jnp.bfloat16)
    return (image_embed_gradient, text_embed_gradient)


def solution(mesh):
    placed = (P(("blk", "grp"), None), P(("blk", "grp"), None))
    return jax.shard_map(
        per_device,
        mesh=mesh,
        in_specs=placed,
        out_specs=(P(("blk", "grp"), None), P(("blk", "grp"), None)),
        check_vma=False,
    )
```

profile of v0, /device:TPU:1, one launch (start us, length us, event | category | flops | bytes accessed | tf_op | source)
XLA Modules:
  0.0 372.6 jit_solution(2720175382725757089)
XLA Ops:
  2.3 367.2 %while.17 = (s32[]{:T(128)}, bf16[128,1152]{1,0:T(8,128)(2,1)S(1)}, bf16[128,1152]{1,0:T(8,128)(2,1)S(1)}, f32[128,1152]{1,0:T(8,128)S(1)}, f32[128,1152]{1,0:T(...) while((s32[]{:T(128)}, bf16[128,1152]{1,0:T(8,128)(2,1)S(1)}, ...), condition=%wide.region_3.4_spmd.clone, body=%wide.region_2.3_spmd.clone.sunk | while | flops 151977984 | bytes 7078111 | solution.py:68
  2.4 4.8 %collective-permute-start = (bf16[128,1152]{1,0:T(8,128)(2,1)S(1)}, bf16[128,1152]{1,0:T(8,128)(2,1)S(1)}, u32[]{:S(2)}, u32[]{:S(2)}) collective-permute-start(bf16[128,1152]{1,0:T(8,128)(2,1)S(1)} %copy.10), channel_id=1, source_target_pairs={{0,1},{1,2},{2,3},{3,4},{4,5},{5,6},{6,7},{7,8},{8,9},{9,10},{10,1... | collective-permute-start | bytes 884744 | tf_op jit(solution)/shard_map/while/body/eval_jaxpr/ppermute | solution.py:14
  7.2 6.1 %collective-permute-start.1 = (bf16[128,1152]{1,0:T(8,128)(2,1)S(1)}, bf16[128,1152]{1,0:T(8,128)(2,1)S(1)}, u32[]{:S(2)}, u32[]{:S(2)}) collective-permute-start(bf16[128,1152]{1,0:T(8,128)(2,1)S(1)} %copy.11), channel_id=1, source_target_pairs={{0,767},{1,0},{2,1},{3,2},{4,3},{5,4},{6,5},{7,6},{8,7},{9,8},{10,... | collective-permute-start | bytes 884744 | tf_op jit(solution)/shard_map/while/body/eval_jaxpr/ppermute | solution.py:14
  15.9 3.1 collective-permute-done
  19.0 4.2 %collective-permute-done.1 = bf16[128,1152]{1,0:T(8,128)(2,1)S(1)} collective-permute-done((bf16[128,1152]{1,0:T(8,128)(2,1)S(1)}, bf16[128,1152]{1,0:T(8,128)(2,1)S(1)}, u32[]{:S(2)}, u32[]{:S(2)}) %collective-permute-start.1) | collective-permute-done | bytes 294944 | tf_op jit(solution)/shard_map/while/body/eval_jaxpr/ppermute | solution.py:14
  23.2 3.6 collective-permute-start
  26.9 3.7 collective-permute-start.1
  34.1 7.8 %collective-permute-done.1 = bf16[128,1152]{1,0:T(8,128)(2,1)S(1)} collective-permute-done((bf16[128,1152]{1,0:T(8,128)(2,1)S(1)}, bf16[128,1152]{1,0:T(8,128)(2,1)S(1)}, u32[]{:S(2)}, u32[]{:S(2)}) %collective-permute-start.1) | collective-permute-done | bytes 294944 | tf_op jit(solution)/shard_map/while/body/eval_jaxpr/ppermute | solution.py:14
  41.9 3.0 collective-permute-start
  45.0 4.3 %collective-permute-start.1 = (bf16[128,1152]{1,0:T(8,128)(2,1)S(1)}, bf16[128,1152]{1,0:T(8,128)(2,1)S(1)}, u32[]{:S(2)}, u32[]{:S(2)}) collective-permute-start(bf16[128,1152]{1,0:T(8,128)(2,1)S(1)} %copy.11), channel_id=1, source_target_pairs={{0,767},{1,0},{2,1},{3,2},{4,3},{5,4},{6,5},{7,6},{8,7},{9,8},{10,... | collective-permute-start | bytes 884744 | tf_op jit(solution)/shard_map/while/body/eval_jaxpr/ppermute | solution.py:14
  52.0 9.4 %collective-permute-done.1 = bf16[128,1152]{1,0:T(8,128)(2,1)S(1)} collective-permute-done((bf16[128,1152]{1,0:T(8,128)(2,1)S(1)}, bf16[128,1152]{1,0:T(8,128)(2,1)S(1)}, u32[]{:S(2)}, u32[]{:S(2)}) %collective-permute-start.1) | collective-permute-done | bytes 294944 | tf_op jit(solution)/shard_map/while/body/eval_jaxpr/ppermute | solution.py:14
  63.7 5.1 %collective-permute-start.1 = (bf16[128,1152]{1,0:T(8,128)(2,1)S(1)}, bf16[128,1152]{1,0:T(8,128)(2,1)S(1)}, u32[]{:S(2)}, u32[]{:S(2)}) collective-permute-start(bf16[128,1152]{1,0:T(8,128)(2,1)S(1)} %copy.11), channel_id=1, source_target_pairs={{0,767},{1,0},{2,1},{3,2},{4,3},{5,4},{6,5},{7,6},{8,7},{9,8},{10,... | collective-permute-start | bytes 884744 | tf_op jit(solution)/shard_map/while/body/eval_jaxpr/ppermute | solution.py:14
  72.4 8.5 %collective-permute-done.1 = bf16[128,1152]{1,0:T(8,128)(2,1)S(1)} collective-permute-done((bf16[128,1152]{1,0:T(8,128)(2,1)S(1)}, bf16[128,1152]{1,0:T(8,128)(2,1)S(1)}, u32[]{:S(2)}, u32[]{:S(2)}) %collective-permute-start.1) | collective-permute-done | bytes 294944 | tf_op jit(solution)/shard_map/while/body/eval_jaxpr/ppermute | solution.py:14
  83.3 5.0 %collective-permute-start.1 = (bf16[128,1152]{1,0:T(8,128)(2,1)S(1)}, bf16[128,1152]{1,0:T(8,128)(2,1)S(1)}, u32[]{:S(2)}, u32[]{:S(2)}) collective-permute-start(bf16[128,1152]{1,0:T(8,128)(2,1)S(1)} %copy.11), channel_id=1, source_target_pairs={{0,767},{1,0},{2,1},{3,2},{4,3},{5,4},{6,5},{7,6},{8,7},{9,8},{10,... | collective-permute-start | bytes 884744 | tf_op jit(solution)/shard_map/while/body/eval_jaxpr/ppermute | solution.py:14
  92.1 8.3 %collective-permute-done.1 = bf16[128,1152]{1,0:T(8,128)(2,1)S(1)} collective-permute-done((bf16[128,1152]{1,0:T(8,128)(2,1)S(1)}, bf16[128,1152]{1,0:T(8,128)(2,1)S(1)}, u32[]{:S(2)}, u32[]{:S(2)}) %collective-permute-start.1) | collective-permute-done | bytes 294944 | tf_op jit(solution)/shard_map/while/body/eval_jaxpr/ppermute | solution.py:14
  102.7 5.1 %collective-permute-start.1 = (bf16[128,1152]{1,0:T(8,128)(2,1)S(1)}, bf16[128,1152]{1,0:T(8,128)(2,1)S(1)}, u32[]{:S(2)}, u32[]{:S(2)}) collective-permute-start(bf16[128,1152]{1,0:T(8,128)(2,1)S(1)} %copy.11), channel_id=1, source_target_pairs={{0,767},{1,0},{2,1},{3,2},{4,3},{5,4},{6,5},{7,6},{8,7},{9,8},{10,... | collective-permute-start | bytes 884744 | tf_op jit(solution)/shard_map/while/body/eval_jaxpr/ppermute | solution.py:14
  111.7 8.0 %collective-permute-done.1 = bf16[128,1152]{1,0:T(8,128)(2,1)S(1)} collective-permute-done((bf16[128,1152]{1,0:T(8,128)(2,1)S(1)}, bf16[128,1152]{1,0:T(8,128)(2,1)S(1)}, u32[]{:S(2)}, u32[]{:S(2)}) %collective-permute-start.1) | collective-permute-done | bytes 294944 | tf_op jit(solution)/shard_map/while/body/eval_jaxpr/ppermute | solution.py:14
  119.8 2.4 collective-permute-start
  122.3 5.0 %collective-permute-start.1 = (bf16[128,1152]{1,0:T(8,128)(2,1)S(1)}, bf16[128,1152]{1,0:T(8,128)(2,1)S(1)}, u32[]{:S(2)}, u32[]{:S(2)}) collective-permute-start(bf16[128,1152]{1,0:T(8,128)(2,1)S(1)} %copy.11), channel_id=1, source_target_pairs={{0,767},{1,0},{2,1},{3,2},{4,3},{5,4},{6,5},{7,6},{8,7},{9,8},{10,... | collective-permute-start | bytes 884744 | tf_op jit(solution)/shard_map/while/body/eval_jaxpr/ppermute | solution.py:14
  131.6 7.7 %collective-permute-done.1 = bf16[128,1152]{1,0:T(8,128)(2,1)S(1)} collective-permute-done((bf16[128,1152]{1,0:T(8,128)(2,1)S(1)}, bf16[128,1152]{1,0:T(8,128)(2,1)S(1)}, u32[]{:S(2)}, u32[]{:S(2)}) %collective-permute-start.1) | collective-permute-done | bytes 294944 | tf_op jit(solution)/shard_map/while/body/eval_jaxpr/ppermute | solution.py:14
  141.4 5.4 %collective-permute-start.1 = (bf16[128,1152]{1,0:T(8,128)(2,1)S(1)}, bf16[128,1152]{1,0:T(8,128)(2,1)S(1)}, u32[]{:S(2)}, u32[]{:S(2)}) collective-permute-start(bf16[128,1152]{1,0:T(8,128)(2,1)S(1)} %copy.11), channel_id=1, source_target_pairs={{0,767},{1,0},{2,1},{3,2},{4,3},{5,4},{6,5},{7,6},{8,7},{9,8},{10,... | collective-permute-start | bytes 884744 | tf_op jit(solution)/shard_map/while/body/eval_jaxpr/ppermute | solution.py:14
  151.5 6.6 %collective-permute-done.1 = bf16[128,1152]{1,0:T(8,128)(2,1)S(1)} collective-permute-done((bf16[128,1152]{1,0:T(8,128)(2,1)S(1)}, bf16[128,1152]{1,0:T(8,128)(2,1)S(1)}, u32[]{:S(2)}, u32[]{:S(2)}) %collective-permute-start.1) | collective-permute-done | bytes 294944 | tf_op jit(solution)/shard_map/while/body/eval_jaxpr/ppermute | solution.py:14
  158.1 3.0 collective-permute-start
  161.2 4.3 %collective-permute-start.1 = (bf16[128,1152]{1,0:T(8,128)(2,1)S(1)}, bf16[128,1152]{1,0:T(8,128)(2,1)S(1)}, u32[]{:S(2)}, u32[]{:S(2)}) collective-permute-start(bf16[128,1152]{1,0:T(8,128)(2,1)S(1)} %copy.11), channel_id=1, source_target_pairs={{0,767},{1,0},{2,1},{3,2},{4,3},{5,4},{6,5},{7,6},{8,7},{9,8},{10,... | collective-permute-start | bytes 884744 | tf_op jit(solution)/shard_map/while/body/eval_jaxpr/ppermute | solution.py:14
  169.6 8.1 %collective-permute-done.1 = bf16[128,1152]{1,0:T(8,128)(2,1)S(1)} collective-permute-done((bf16[128,1152]{1,0:T(8,128)(2,1)S(1)}, bf16[128,1152]{1,0:T(8,128)(2,1)S(1)}, u32[]{:S(2)}, u32[]{:S(2)}) %collective-permute-start.1) | collective-permute-done | bytes 294944 | tf_op jit(solution)/shard_map/while/body/eval_jaxpr/ppermute | solution.py:14
  179.9 5.2 %collective-permute-start.1 = (bf16[128,1152]{1,0:T(8,128)(2,1)S(1)}, bf16[128,1152]{1,0:T(8,128)(2,1)S(1)}, u32[]{:S(2)}, u32[]{:S(2)}) collective-permute-start(bf16[128,1152]{1,0:T(8,128)(2,1)S(1)} %copy.11), channel_id=1, source_target_pairs={{0,767},{1,0},{2,1},{3,2},{4,3},{5,4},{6,5},{7,6},{8,7},{9,8},{10,... | collective-permute-start | bytes 884744 | tf_op jit(solution)/shard_map/while/body/eval_jaxpr/ppermute | solution.py:14
  189.7 7.2 %collective-permute-done.1 = bf16[128,1152]{1,0:T(8,128)(2,1)S(1)} collective-permute-done((bf16[128,1152]{1,0:T(8,128)(2,1)S(1)}, bf16[128,1152]{1,0:T(8,128)(2,1)S(1)}, u32[]{:S(2)}, u32[]{:S(2)}) %collective-permute-start.1) | collective-permute-done | bytes 294944 | tf_op jit(solution)/shard_map/while/body/eval_jaxpr/ppermute | solution.py:14
  198.9 5.4 %collective-permute-start.1 = (bf16[128,1152]{1,0:T(8,128)(2,1)S(1)}, bf16[128,1152]{1,0:T(8,128)(2,1)S(1)}, u32[]{:S(2)}, u32[]{:S(2)}) collective-permute-start(bf16[128,1152]{1,0:T(8,128)(2,1)S(1)} %copy.11), channel_id=1, source_target_pairs={{0,767},{1,0},{2,1},{3,2},{4,3},{5,4},{6,5},{7,6},{8,7},{9,8},{10,... | collective-permute-start | bytes 884744 | tf_op jit(solution)/shard_map/while/body/eval_jaxpr/ppermute | solution.py:14
  209.1 6.5 %collective-permute-done.1 = bf16[128,1152]{1,0:T(8,128)(2,1)S(1)} collective-permute-done((bf16[128,1152]{1,0:T(8,128)(2,1)S(1)}, bf16[128,1152]{1,0:T(8,128)(2,1)S(1)}, u32[]{:S(2)}, u32[]{:S(2)}) %collective-permute-start.1) | collective-permute-done | bytes 294944 | tf_op jit(solution)/shard_map/while/body/eval_jaxpr/ppermute | solution.py:14
  215.7 3.1 collective-permute-start
  218.8 4.3 %collective-permute-start.1 = (bf16[128,1152]{1,0:T(8,128)(2,1)S(1)}, bf16[128,1152]{1,0:T(8,128)(2,1)S(1)}, u32[]{:S(2)}, u32[]{:S(2)}) collective-permute-start(bf16[128,1152]{1,0:T(8,128)(2,1)S(1)} %copy.11), channel_id=1, source_target_pairs={{0,767},{1,0},{2,1},{3,2},{4,3},{5,4},{6,5},{7,6},{8,7},{9,8},{10,... | collective-permute-start | bytes 884744 | tf_op jit(solution)/shard_map/while/body/eval_jaxpr/ppermute | solution.py:14
  227.1 8.1 %collective-permute-done.1 = bf16[128,1152]{1,0:T(8,128)(2,1)S(1)} collective-permute-done((bf16[128,1152]{1,0:T(8,128)(2,1)S(1)}, bf16[128,1152]{1,0:T(8,128)(2,1)S(1)}, u32[]{:S(2)}, u32[]{:S(2)}) %collective-permute-start.1) | collective-permute-done | bytes 294944 | tf_op jit(solution)/shard_map/while/body/eval_jaxpr/ppermute | solution.py:14
  237.4 5.2 %collective-permute-start.1 = (bf16[128,1152]{1,0:T(8,128)(2,1)S(1)}, bf16[128,1152]{1,0:T(8,128)(2,1)S(1)}, u32[]{:S(2)}, u32[]{:S(2)}) collective-permute-start(bf16[128,1152]{1,0:T(8,128)(2,1)S(1)} %copy.11), channel_id=1, source_target_pairs={{0,767},{1,0},{2,1},{3,2},{4,3},{5,4},{6,5},{7,6},{8,7},{9,8},{10,... | collective-permute-start | bytes 884744 | tf_op jit(solution)/shard_map/while/body/eval_jaxpr/ppermute | solution.py:14
  247.3 7.2 %collective-permute-done.1 = bf16[128,1152]{1,0:T(8,128)(2,1)S(1)} collective-permute-done((bf16[128,1152]{1,0:T(8,128)(2,1)S(1)}, bf16[128,1152]{1,0:T(8,128)(2,1)S(1)}, u32[]{:S(2)}, u32[]{:S(2)}) %collective-permute-start.1) | collective-permute-done | bytes 294944 | tf_op jit(solution)/shard_map/while/body/eval_jaxpr/ppermute | solution.py:14
  256.4 5.4 %collective-permute-start.1 = (bf16[128,1152]{1,0:T(8,128)(2,1)S(1)}, bf16[128,1152]{1,0:T(8,128)(2,1)S(1)}, u32[]{:S(2)}, u32[]{:S(2)}) collective-permute-start(bf16[128,1152]{1,0:T(8,128)(2,1)S(1)} %copy.11), channel_id=1, source_target_pairs={{0,767},{1,0},{2,1},{3,2},{4,3},{5,4},{6,5},{7,6},{8,7},{9,8},{10,... | collective-permute-start | bytes 884744 | tf_op jit(solution)/shard_map/while/body/eval_jaxpr/ppermute | solution.py:14
  266.6 6.6 %collective-permute-done.1 = bf16[128,1152]{1,0:T(8,128)(2,1)S(1)} collective-permute-done((bf16[128,1152]{1,0:T(8,128)(2,1)S(1)}, bf16[128,1152]{1,0:T(8,128)(2,1)S(1)}, u32[]{:S(2)}, u32[]{:S(2)}) %collective-permute-start.1) | collective-permute-done | bytes 294944 | tf_op jit(solution)/shard_map/while/body/eval_jaxpr/ppermute | solution.py:14
  273.2 3.1 collective-permute-start
  276.3 4.3 %collective-permute-start.1 = (bf16[128,1152]{1,0:T(8,128)(2,1)S(1)}, bf16[128,1152]{1,0:T(8,128)(2,1)S(1)}, u32[]{:S(2)}, u32[]{:S(2)}) collective-permute-start(bf16[128,1152]{1,0:T(8,128)(2,1)S(1)} %copy.11), channel_id=1, source_target_pairs={{0,767},{1,0},{2,1},{3,2},{4,3},{5,4},{6,5},{7,6},{8,7},{9,8},{10,... | collective-permute-start | bytes 884744 | tf_op jit(solution)/shard_map/while/body/eval_jaxpr/ppermute | solution.py:14
  284.6 8.1 %collective-permute-done.1 = bf16[128,1152]{1,0:T(8,128)(2,1)S(1)} collective-permute-done((bf16[128,1152]{1,0:T(8,128)(2,1)S(1)}, bf16[128,1152]{1,0:T(8,128)(2,1)S(1)}, u32[]{:S(2)}, u32[]{:S(2)}) %collective-permute-start.1) | collective-permute-done | bytes 294944 | tf_op jit(solution)/shard_map/while/body/eval_jaxpr/ppermute | solution.py:14
  295.0 5.2 %collective-permute-start.1 = (bf16[128,1152]{1,0:T(8,128)(2,1)S(1)}, bf16[128,1152]{1,0:T(8,128)(2,1)S(1)}, u32[]{:S(2)}, u32[]{:S(2)}) collective-permute-start(bf16[128,1152]{1,0:T(8,128)(2,1)S(1)} %copy.11), channel_id=1, source_target_pairs={{0,767},{1,0},{2,1},{3,2},{4,3},{5,4},{6,5},{7,6},{8,7},{9,8},{10,... | collective-permute-start | bytes 884744 | tf_op jit(solution)/shard_map/while/body/eval_jaxpr/ppermute | solution.py:14
  304.8 7.2 %collective-permute-done.1 = bf16[128,1152]{1,0:T(8,128)(2,1)S(1)} collective-permute-done((bf16[128,1152]{1,0:T(8,128)(2,1)S(1)}, bf16[128,1152]{1,0:T(8,128)(2,1)S(1)}, u32[]{:S(2)}, u32[]{:S(2)}) %collective-permute-start.1) | collective-permute-done | bytes 294944 | tf_op jit(solution)/shard_map/while/body/eval_jaxpr/ppermute | solution.py:14
  314.0 5.4 %collective-permute-start.1 = (bf16[128,1152]{1,0:T(8,128)(2,1)S(1)}, bf16[128,1152]{1,0:T(8,128)(2,1)S(1)}, u32[]{:S(2)}, u32[]{:S(2)}) collective-permute-start(bf16[128,1152]{1,0:T(8,128)(2,1)S(1)} %copy.11), channel_id=1, source_target_pairs={{0,767},{1,0},{2,1},{3,2},{4,3},{5,4},{6,5},{7,6},{8,7},{9,8},{10,... | collective-permute-start | bytes 884744 | tf_op jit(solution)/shard_map/while/body/eval_jaxpr/ppermute | solution.py:14
  324.1 6.6 %collective-permute-done.1 = bf16[128,1152]{1,0:T(8,128)(2,1)S(1)} collective-permute-done((bf16[128,1152]{1,0:T(8,128)(2,1)S(1)}, bf16[128,1152]{1,0:T(8,128)(2,1)S(1)}, u32[]{:S(2)}, u32[]{:S(2)}) %collective-permute-start.1) | collective-permute-done | bytes 294944 | tf_op jit(solution)/shard_map/while/body/eval_jaxpr/ppermute | solution.py:14
  330.7 3.1 collective-permute-start
  333.8 4.3 %collective-permute-start.1 = (bf16[128,1152]{1,0:T(8,128)(2,1)S(1)}, bf16[128,1152]{1,0:T(8,128)(2,1)S(1)}, u32[]{:S(2)}, u32[]{:S(2)}) collective-permute-start(bf16[128,1152]{1,0:T(8,128)(2,1)S(1)} %copy.11), channel_id=1, source_target_pairs={{0,767},{1,0},{2,1},{3,2},{4,3},{5,4},{6,5},{7,6},{8,7},{9,8},{10,... | collective-permute-start | bytes 884744 | tf_op jit(solution)/shard_map/while/body/eval_jaxpr/ppermute | solution.py:14
  342.1 8.1 %collective-permute-done.1 = bf16[128,1152]{1,0:T(8,128)(2,1)S(1)} collective-permute-done((bf16[128,1152]{1,0:T(8,128)(2,1)S(1)}, bf16[128,1152]{1,0:T(8,128)(2,1)S(1)}, u32[]{:S(2)}, u32[]{:S(2)}) %collective-permute-start.1) | collective-permute-done | bytes 294944 | tf_op jit(solution)/shard_map/while/body/eval_jaxpr/ppermute | solution.py:14
  352.5 5.2 %collective-permute-start.1 = (bf16[128,1152]{1,0:T(8,128)(2,1)S(1)}, bf16[128,1152]{1,0:T(8,128)(2,1)S(1)}, u32[]{:S(2)}, u32[]{:S(2)}) collective-permute-start(bf16[128,1152]{1,0:T(8,128)(2,1)S(1)} %copy.11), channel_id=1, source_target_pairs={{0,767},{1,0},{2,1},{3,2},{4,3},{5,4},{6,5},{7,6},{8,7},{9,8},{10,... | collective-permute-start | bytes 884744 | tf_op jit(solution)/shard_map/while/body/eval_jaxpr/ppermute | solution.py:14
  362.3 7.2 %collective-permute-done.1 = bf16[128,1152]{1,0:T(8,128)(2,1)S(1)} collective-permute-done((bf16[128,1152]{1,0:T(8,128)(2,1)S(1)}, bf16[128,1152]{1,0:T(8,128)(2,1)S(1)}, u32[]{:S(2)}, u32[]{:S(2)}) %collective-permute-start.1) | collective-permute-done | bytes 294944 | tf_op jit(solution)/shard_map/while/body/eval_jaxpr/ppermute | solution.py:14
  (142 shorter events, 94.3 us)
Async XLA Ops:
  0.6 1.2 copy-start.1
  0.6 1.4 copy-start
  2.4 16.6 %collective-permute-start = (bf16[128,1152]{1,0:T(8,128)(2,1)S(1)}, bf16[128,1152]{1,0:T(8,128)(2,1)S(1)}, u32[]{:S(2)}, u32[]{:S(2)}) collective-permute-start(bf16[128,1152]{1,0:T(8,128)(2,1)S(1)} %copy.10), channel_id=1, source_target_pairs={{0,1},{1,2},{2,3},{3,4},{4,5},{5,6},{6,7},{7,8},{8,9},{9,10},{10,1... | collective-permute-start | bytes 884744 | tf_op jit(solution)/shard_map/while/body/eval_jaxpr/ppermute | solution.py:14
  7.2 15.9 %collective-permute-start.1 = (bf16[128,1152]{1,0:T(8,128)(2,1)S(1)}, bf16[128,1152]{1,0:T(8,128)(2,1)S(1)}, u32[]{:S(2)}, u32[]{:S(2)}) collective-permute-start(bf16[128,1152]{1,0:T(8,128)(2,1)S(1)} %copy.11), channel_id=1, source_target_pairs={{0,767},{1,0},{2,1},{3,2},{4,3},{5,4},{6,5},{7,6},{8,7},{9,8},{10,... | collective-permute-start | bytes 884744 | tf_op jit(solution)/shard_map/while/body/eval_jaxpr/ppermute | solution.py:14
  23.2 10.9 %collective-permute-start = (bf16[128,1152]{1,0:T(8,128)(2,1)S(1)}, bf16[128,1152]{1,0:T(8,128)(2,1)S(1)}, u32[]{:S(2)}, u32[]{:S(2)}) collective-permute-start(bf16[128,1152]{1,0:T(8,128)(2,1)S(1)} %copy.10), channel_id=1, source_target_pairs={{0,1},{1,2},{2,3},{3,4},{4,5},{5,6},{6,7},{7,8},{8,9},{9,10},{10,1... | collective-permute-start | bytes 884744 | tf_op jit(solution)/shard_map/while/body/eval_jaxpr/ppermute | solution.py:14
  26.9 15.0 %collective-permute-start.1 = (bf16[128,1152]{1,0:T(8,128)(2,1)S(1)}, bf16[128,1152]{1,0:T(8,128)(2,1)S(1)}, u32[]{:S(2)}, u32[]{:S(2)}) collective-permute-start(bf16[128,1152]{1,0:T(8,128)(2,1)S(1)} %copy.11), channel_id=1, source_target_pairs={{0,767},{1,0},{2,1},{3,2},{4,3},{5,4},{6,5},{7,6},{8,7},{9,8},{10,... | collective-permute-start | bytes 884744 | tf_op jit(solution)/shard_map/while/body/eval_jaxpr/ppermute | solution.py:14
  41.9 10.1 %collective-permute-start = (bf16[128,1152]{1,0:T(8,128)(2,1)S(1)}, bf16[128,1152]{1,0:T(8,128)(2,1)S(1)}, u32[]{:S(2)}, u32[]{:S(2)}) collective-permute-start(bf16[128,1152]{1,0:T(8,128)(2,1)S(1)} %copy.10), channel_id=1, source_target_pairs={{0,1},{1,2},{2,3},{3,4},{4,5},{5,6},{6,7},{7,8},{8,9},{9,10},{10,1... | collective-permute-start | bytes 884744 | tf_op jit(solution)/shard_map/while/body/eval_jaxpr/ppermute | solution.py:14
  45.0 16.4 %collective-permute-start.1 = (bf16[128,1152]{1,0:T(8,128)(2,1)S(1)}, bf16[128,1152]{1,0:T(8,128)(2,1)S(1)}, u32[]{:S(2)}, u32[]{:S(2)}) collective-permute-start(bf16[128,1152]{1,0:T(8,128)(2,1)S(1)} %copy.11), channel_id=1, source_target_pairs={{0,767},{1,0},{2,1},{3,2},{4,3},{5,4},{6,5},{7,6},{8,7},{9,8},{10,... | collective-permute-start | bytes 884744 | tf_op jit(solution)/shard_map/while/body/eval_jaxpr/ppermute | solution.py:14
  61.4 10.9 %collective-permute-start = (bf16[128,1152]{1,0:T(8,128)(2,1)S(1)}, bf16[128,1152]{1,0:T(8,128)(2,1)S(1)}, u32[]{:S(2)}, u32[]{:S(2)}) collective-permute-start(bf16[128,1152]{1,0:T(8,128)(2,1)S(1)} %copy.10), channel_id=1, source_target_pairs={{0,1},{1,2},{2,3},{3,4},{4,5},{5,6},{6,7},{7,8},{8,9},{9,10},{10,1... | collective-permute-start | bytes 884744 | tf_op jit(solution)/shard_map/while/body/eval_jaxpr/ppermute | solution.py:14
  63.7 17.1 %collective-permute-start.1 = (bf16[128,1152]{1,0:T(8,128)(2,1)S(1)}, bf16[128,1152]{1,0:T(8,128)(2,1)S(1)}, u32[]{:S(2)}, u32[]{:S(2)}) collective-permute-start(bf16[128,1152]{1,0:T(8,128)(2,1)S(1)} %copy.11), channel_id=1, source_target_pairs={{0,767},{1,0},{2,1},{3,2},{4,3},{5,4},{6,5},{7,6},{8,7},{9,8},{10,... | collective-permute-start | bytes 884744 | tf_op jit(solution)/shard_map/while/body/eval_jaxpr/ppermute | solution.py:14
  80.9 11.2 %collective-permute-start = (bf16[128,1152]{1,0:T(8,128)(2,1)S(1)}, bf16[128,1152]{1,0:T(8,128)(2,1)S(1)}, u32[]{:S(2)}, u32[]{:S(2)}) collective-permute-start(bf16[128,1152]{1,0:T(8,128)(2,1)S(1)} %copy.10), channel_id=1, source_target_pairs={{0,1},{1,2},{2,3},{3,4},{4,5},{5,6},{6,7},{7,8},{8,9},{9,10},{10,1... | collective-permute-start | bytes 884744 | tf_op jit(solution)/shard_map/while/body/eval_jaxpr/ppermute | solution.py:14
  83.3 17.1 %collective-permute-start.1 = (bf16[128,1152]{1,0:T(8,128)(2,1)S(1)}, bf16[128,1152]{1,0:T(8,128)(2,1)S(1)}, u32[]{:S(2)}, u32[]{:S(2)}) collective-permute-start(bf16[128,1152]{1,0:T(8,128)(2,1)S(1)} %copy.11), channel_id=1, source_target_pairs={{0,767},{1,0},{2,1},{3,2},{4,3},{5,4},{6,5},{7,6},{8,7},{9,8},{10,... | collective-permute-start | bytes 884744 | tf_op jit(solution)/shard_map/while/body/eval_jaxpr/ppermute | solution.py:14
  100.4 11.3 %collective-permute-start = (bf16[128,1152]{1,0:T(8,128)(2,1)S(1)}, bf16[128,1152]{1,0:T(8,128)(2,1)S(1)}, u32[]{:S(2)}, u32[]{:S(2)}) collective-permute-start(bf16[128,1152]{1,0:T(8,128)(2,1)S(1)} %copy.10), channel_id=1, source_target_pairs={{0,1},{1,2},{2,3},{3,4},{4,5},{5,6},{6,7},{7,8},{8,9},{9,10},{10,1... | collective-permute-start | bytes 884744 | tf_op jit(solution)/shard_map/while/body/eval_jaxpr/ppermute | solution.py:14
  102.7 17.1 %collective-permute-start.1 = (bf16[128,1152]{1,0:T(8,128)(2,1)S(1)}, bf16[128,1152]{1,0:T(8,128)(2,1)S(1)}, u32[]{:S(2)}, u32[]{:S(2)}) collective-permute-start(bf16[128,1152]{1,0:T(8,128)(2,1)S(1)} %copy.11), channel_id=1, source_target_pairs={{0,767},{1,0},{2,1},{3,2},{4,3},{5,4},{6,5},{7,6},{8,7},{9,8},{10,... | collective-permute-start | bytes 884744 | tf_op jit(solution)/shard_map/while/body/eval_jaxpr/ppermute | solution.py:14
  119.8 11.8 %collective-permute-start = (bf16[128,1152]{1,0:T(8,128)(2,1)S(1)}, bf16[128,1152]{1,0:T(8,128)(2,1)S(1)}, u32[]{:S(2)}, u32[]{:S(2)}) collective-permute-start(bf16[128,1152]{1,0:T(8,128)(2,1)S(1)} %copy.10), channel_id=1, source_target_pairs={{0,1},{1,2},{2,3},{3,4},{4,5},{5,6},{6,7},{7,8},{8,9},{9,10},{10,1... | collective-permute-start | bytes 884744 | tf_op jit(solution)/shard_map/while/body/eval_jaxpr/ppermute | solution.py:14
  122.3 17.1 %collective-permute-start.1 = (bf16[128,1152]{1,0:T(8,128)(2,1)S(1)}, bf16[128,1152]{1,0:T(8,128)(2,1)S(1)}, u32[]{:S(2)}, u32[]{:S(2)}) collective-permute-start(bf16[128,1152]{1,0:T(8,128)(2,1)S(1)} %copy.11), channel_id=1, source_target_pairs={{0,767},{1,0},{2,1},{3,2},{4,3},{5,4},{6,5},{7,6},{8,7},{9,8},{10,... | collective-permute-start | bytes 884744 | tf_op jit(solution)/shard_map/while/body/eval_jaxpr/ppermute | solution.py:14
  139.4 12.1 %collective-permute-start = (bf16[128,1152]{1,0:T(8,128)(2,1)S(1)}, bf16[128,1152]{1,0:T(8,128)(2,1)S(1)}, u32[]{:S(2)}, u32[]{:S(2)}) collective-permute-start(bf16[128,1152]{1,0:T(8,128)(2,1)S(1)} %copy.10), channel_id=1, source_target_pairs={{0,1},{1,2},{2,3},{3,4},{4,5},{5,6},{6,7},{7,8},{8,9},{9,10},{10,1... | collective-permute-start | bytes 884744 | tf_op jit(solution)/shard_map/while/body/eval_jaxpr/ppermute | solution.py:14
  141.4 16.7 %collective-permute-start.1 = (bf16[128,1152]{1,0:T(8,128)(2,1)S(1)}, bf16[128,1152]{1,0:T(8,128)(2,1)S(1)}, u32[]{:S(2)}, u32[]{:S(2)}) collective-permute-start(bf16[128,1152]{1,0:T(8,128)(2,1)S(1)} %copy.11), channel_id=1, source_target_pairs={{0,767},{1,0},{2,1},{3,2},{4,3},{5,4},{6,5},{7,6},{8,7},{9,8},{10,... | collective-permute-start | bytes 884744 | tf_op jit(solution)/shard_map/while/body/eval_jaxpr/ppermute | solution.py:14
  158.1 11.5 %collective-permute-start = (bf16[128,1152]{1,0:T(8,128)(2,1)S(1)}, bf16[128,1152]{1,0:T(8,128)(2,1)S(1)}, u32[]{:S(2)}, u32[]{:S(2)}) collective-permute-start(bf16[128,1152]{1,0:T(8,128)(2,1)S(1)} %copy.10), channel_id=1, source_target_pairs={{0,1},{1,2},{2,3},{3,4},{4,5},{5,6},{6,7},{7,8},{8,9},{9,10},{10,1... | collective-permute-start | bytes 884744 | tf_op jit(solution)/shard_map/while/body/eval_jaxpr/ppermute | solution.py:14
  161.2 16.4 %collective-permute-start.1 = (bf16[128,1152]{1,0:T(8,128)(2,1)S(1)}, bf16[128,1152]{1,0:T(8,128)(2,1)S(1)}, u32[]{:S(2)}, u32[]{:S(2)}) collective-permute-start(bf16[128,1152]{1,0:T(8,128)(2,1)S(1)} %copy.11), channel_id=1, source_target_pairs={{0,767},{1,0},{2,1},{3,2},{4,3},{5,4},{6,5},{7,6},{8,7},{9,8},{10,... | collective-permute-start | bytes 884744 | tf_op jit(solution)/shard_map/while/body/eval_jaxpr/ppermute | solution.py:14
  177.7 12.1 %collective-permute-start = (bf16[128,1152]{1,0:T(8,128)(2,1)S(1)}, bf16[128,1152]{1,0:T(8,128)(2,1)S(1)}, u32[]{:S(2)}, u32[]{:S(2)}) collective-permute-start(bf16[128,1152]{1,0:T(8,128)(2,1)S(1)} %copy.10), channel_id=1, source_target_pairs={{0,1},{1,2},{2,3},{3,4},{4,5},{5,6},{6,7},{7,8},{8,9},{9,10},{10,1... | collective-permute-start | bytes 884744 | tf_op jit(solution)/shard_map/while/body/eval_jaxpr/ppermute | solution.py:14
  179.9 17.0 %collective-permute-start.1 = (bf16[128,1152]{1,0:T(8,128)(2,1)S(1)}, bf16[128,1152]{1,0:T(8,128)(2,1)S(1)}, u32[]{:S(2)}, u32[]{:S(2)}) collective-permute-start(bf16[128,1152]{1,0:T(8,128)(2,1)S(1)} %copy.11), channel_id=1, source_target_pairs={{0,767},{1,0},{2,1},{3,2},{4,3},{5,4},{6,5},{7,6},{8,7},{9,8},{10,... | collective-permute-start | bytes 884744 | tf_op jit(solution)/shard_map/while/body/eval_jaxpr/ppermute | solution.py:14
  196.9 12.2 %collective-permute-start = (bf16[128,1152]{1,0:T(8,128)(2,1)S(1)}, bf16[128,1152]{1,0:T(8,128)(2,1)S(1)}, u32[]{:S(2)}, u32[]{:S(2)}) collective-permute-start(bf16[128,1152]{1,0:T(8,128)(2,1)S(1)} %copy.10), channel_id=1, source_target_pairs={{0,1},{1,2},{2,3},{3,4},{4,5},{5,6},{6,7},{7,8},{8,9},{9,10},{10,1... | collective-permute-start | bytes 884744 | tf_op jit(solution)/shard_map/while/body/eval_jaxpr/ppermute | solution.py:14
  198.9 16.7 %collective-permute-start.1 = (bf16[128,1152]{1,0:T(8,128)(2,1)S(1)}, bf16[128,1152]{1,0:T(8,128)(2,1)S(1)}, u32[]{:S(2)}, u32[]{:S(2)}) collective-permute-start(bf16[128,1152]{1,0:T(8,128)(2,1)S(1)} %copy.11), channel_id=1, source_target_pairs={{0,767},{1,0},{2,1},{3,2},{4,3},{5,4},{6,5},{7,6},{8,7},{9,8},{10,... | collective-permute-start | bytes 884744 | tf_op jit(solution)/shard_map/while/body/eval_jaxpr/ppermute | solution.py:14
  215.7 11.5 %collective-permute-start = (bf16[128,1152]{1,0:T(8,128)(2,1)S(1)}, bf16[128,1152]{1,0:T(8,128)(2,1)S(1)}, u32[]{:S(2)}, u32[]{:S(2)}) collective-permute-start(bf16[128,1152]{1,0:T(8,128)(2,1)S(1)} %copy.10), channel_id=1, source_target_pairs={{0,1},{1,2},{2,3},{3,4},{4,5},{5,6},{6,7},{7,8},{8,9},{9,10},{10,1... | collective-permute-start | bytes 884744 | tf_op jit(solution)/shard_map/while/body/eval_jaxpr/ppermute | solution.py:14
  218.8 16.4 %collective-permute-start.1 = (bf16[128,1152]{1,0:T(8,128)(2,1)S(1)}, bf16[128,1152]{1,0:T(8,128)(2,1)S(1)}, u32[]{:S(2)}, u32[]{:S(2)}) collective-permute-start(bf16[128,1152]{1,0:T(8,128)(2,1)S(1)} %copy.11), channel_id=1, source_target_pairs={{0,767},{1,0},{2,1},{3,2},{4,3},{5,4},{6,5},{7,6},{8,7},{9,8},{10,... | collective-permute-start | bytes 884744 | tf_op jit(solution)/shard_map/while/body/eval_jaxpr/ppermute | solution.py:14
  235.2 12.0 %collective-permute-start = (bf16[128,1152]{1,0:T(8,128)(2,1)S(1)}, bf16[128,1152]{1,0:T(8,128)(2,1)S(1)}, u32[]{:S(2)}, u32[]{:S(2)}) collective-permute-start(bf16[128,1152]{1,0:T(8,128)(2,1)S(1)} %copy.10), channel_id=1, source_target_pairs={{0,1},{1,2},{2,3},{3,4},{4,5},{5,6},{6,7},{7,8},{8,9},{9,10},{10,1... | collective-permute-start | bytes 884744 | tf_op jit(solution)/shard_map/while/body/eval_jaxpr/ppermute | solution.py:14
  237.4 17.0 %collective-permute-start.1 = (bf16[128,1152]{1,0:T(8,128)(2,1)S(1)}, bf16[128,1152]{1,0:T(8,128)(2,1)S(1)}, u32[]{:S(2)}, u32[]{:S(2)}) collective-permute-start(bf16[128,1152]{1,0:T(8,128)(2,1)S(1)} %copy.11), channel_id=1, source_target_pairs={{0,767},{1,0},{2,1},{3,2},{4,3},{5,4},{6,5},{7,6},{8,7},{9,8},{10,... | collective-permute-start | bytes 884744 | tf_op jit(solution)/shard_map/while/body/eval_jaxpr/ppermute | solution.py:14
  254.5 12.1 %collective-permute-start = (bf16[128,1152]{1,0:T(8,128)(2,1)S(1)}, bf16[128,1152]{1,0:T(8,128)(2,1)S(1)}, u32[]{:S(2)}, u32[]{:S(2)}) collective-permute-start(bf16[128,1152]{1,0:T(8,128)(2,1)S(1)} %copy.10), channel_id=1, source_target_pairs={{0,1},{1,2},{2,3},{3,4},{4,5},{5,6},{6,7},{7,8},{8,9},{9,10},{10,1... | collective-permute-start | bytes 884744 | tf_op jit(solution)/shard_map/while/body/eval_jaxpr/ppermute | solution.py:14
  256.4 16.7 %collective-permute-start.1 = (bf16[128,1152]{1,0:T(8,128)(2,1)S(1)}, bf16[128,1152]{1,0:T(8,128)(2,1)S(1)}, u32[]{:S(2)}, u32[]{:S(2)}) collective-permute-start(bf16[128,1152]{1,0:T(8,128)(2,1)S(1)} %copy.11), channel_id=1, source_target_pairs={{0,767},{1,0},{2,1},{3,2},{4,3},{5,4},{6,5},{7,6},{8,7},{9,8},{10,... | collective-permute-start | bytes 884744 | tf_op jit(solution)/shard_map/while/body/eval_jaxpr/ppermute | solution.py:14
  273.2 11.4 %collective-permute-start = (bf16[128,1152]{1,0:T(8,128)(2,1)S(1)}, bf16[128,1152]{1,0:T(8,128)(2,1)S(1)}, u32[]{:S(2)}, u32[]{:S(2)}) collective-permute-start(bf16[128,1152]{1,0:T(8,128)(2,1)S(1)} %copy.10), channel_id=1, source_target_pairs={{0,1},{1,2},{2,3},{3,4},{4,5},{5,6},{6,7},{7,8},{8,9},{9,10},{10,1... | collective-permute-start | bytes 884744 | tf_op jit(solution)/shard_map/while/body/eval_jaxpr/ppermute | solution.py:14
  276.3 16.4 %collective-permute-start.1 = (bf16[128,1152]{1,0:T(8,128)(2,1)S(1)}, bf16[128,1152]{1,0:T(8,128)(2,1)S(1)}, u32[]{:S(2)}, u32[]{:S(2)}) collective-permute-start(bf16[128,1152]{1,0:T(8,128)(2,1)S(1)} %copy.11), channel_id=1, source_target_pairs={{0,767},{1,0},{2,1},{3,2},{4,3},{5,4},{6,5},{7,6},{8,7},{9,8},{10,... | collective-permute-start | bytes 884744 | tf_op jit(solution)/shard_map/while/body/eval_jaxpr/ppermute | solution.py:14
  292.7 12.1 %collective-permute-start = (bf16[128,1152]{1,0:T(8,128)(2,1)S(1)}, bf16[128,1152]{1,0:T(8,128)(2,1)S(1)}, u32[]{:S(2)}, u32[]{:S(2)}) collective-permute-start(bf16[128,1152]{1,0:T(8,128)(2,1)S(1)} %copy.10), channel_id=1, source_target_pairs={{0,1},{1,2},{2,3},{3,4},{4,5},{5,6},{6,7},{7,8},{8,9},{9,10},{10,1... | collective-permute-start | bytes 884744 | tf_op jit(solution)/shard_map/while/body/eval_jaxpr/ppermute | solution.py:14
  295.0 17.0 %collective-permute-start.1 = (bf16[128,1152]{1,0:T(8,128)(2,1)S(1)}, bf16[128,1152]{1,0:T(8,128)(2,1)S(1)}, u32[]{:S(2)}, u32[]{:S(2)}) collective-permute-start(bf16[128,1152]{1,0:T(8,128)(2,1)S(1)} %copy.11), channel_id=1, source_target_pairs={{0,767},{1,0},{2,1},{3,2},{4,3},{5,4},{6,5},{7,6},{8,7},{9,8},{10,... | collective-permute-start | bytes 884744 | tf_op jit(solution)/shard_map/while/body/eval_jaxpr/ppermute | solution.py:14
  312.0 12.1 %collective-permute-start = (bf16[128,1152]{1,0:T(8,128)(2,1)S(1)}, bf16[128,1152]{1,0:T(8,128)(2,1)S(1)}, u32[]{:S(2)}, u32[]{:S(2)}) collective-permute-start(bf16[128,1152]{1,0:T(8,128)(2,1)S(1)} %copy.10), channel_id=1, source_target_pairs={{0,1},{1,2},{2,3},{3,4},{4,5},{5,6},{6,7},{7,8},{8,9},{9,10},{10,1... | collective-permute-start | bytes 884744 | tf_op jit(solution)/shard_map/while/body/eval_jaxpr/ppermute | solution.py:14
  314.0 16.7 %collective-permute-start.1 = (bf16[128,1152]{1,0:T(8,128)(2,1)S(1)}, bf16[128,1152]{1,0:T(8,128)(2,1)S(1)}, u32[]{:S(2)}, u32[]{:S(2)}) collective-permute-start(bf16[128,1152]{1,0:T(8,128)(2,1)S(1)} %copy.11), channel_id=1, source_target_pairs={{0,767},{1,0},{2,1},{3,2},{4,3},{5,4},{6,5},{7,6},{8,7},{9,8},{10,... | collective-permute-start | bytes 884744 | tf_op jit(solution)/shard_map/while/body/eval_jaxpr/ppermute | solution.py:14
  330.7 11.4 %collective-permute-start = (bf16[128,1152]{1,0:T(8,128)(2,1)S(1)}, bf16[128,1152]{1,0:T(8,128)(2,1)S(1)}, u32[]{:S(2)}, u32[]{:S(2)}) collective-permute-start(bf16[128,1152]{1,0:T(8,128)(2,1)S(1)} %copy.10), channel_id=1, source_target_pairs={{0,1},{1,2},{2,3},{3,4},{4,5},{5,6},{6,7},{7,8},{8,9},{9,10},{10,1... | collective-permute-start | bytes 884744 | tf_op jit(solution)/shard_map/while/body/eval_jaxpr/ppermute | solution.py:14
  333.8 16.4 %collective-permute-start.1 = (bf16[128,1152]{1,0:T(8,128)(2,1)S(1)}, bf16[128,1152]{1,0:T(8,128)(2,1)S(1)}, u32[]{:S(2)}, u32[]{:S(2)}) collective-permute-start(bf16[128,1152]{1,0:T(8,128)(2,1)S(1)} %copy.11), channel_id=1, source_target_pairs={{0,767},{1,0},{2,1},{3,2},{4,3},{5,4},{6,5},{7,6},{8,7},{9,8},{10,... | collective-permute-start | bytes 884744 | tf_op jit(solution)/shard_map/while/body/eval_jaxpr/ppermute | solution.py:14
  350.3 12.1 %collective-permute-start = (bf16[128,1152]{1,0:T(8,128)(2,1)S(1)}, bf16[128,1152]{1,0:T(8,128)(2,1)S(1)}, u32[]{:S(2)}, u32[]{:S(2)}) collective-permute-start(bf16[128,1152]{1,0:T(8,128)(2,1)S(1)} %copy.10), channel_id=1, source_target_pairs={{0,1},{1,2},{2,3},{3,4},{4,5},{5,6},{6,7},{7,8},{8,9},{9,10},{10,1... | collective-permute-start | bytes 884744 | tf_op jit(solution)/shard_map/while/body/eval_jaxpr/ppermute | solution.py:14
  352.5 17.0 %collective-permute-start.1 = (bf16[128,1152]{1,0:T(8,128)(2,1)S(1)}, bf16[128,1152]{1,0:T(8,128)(2,1)S(1)}, u32[]{:S(2)}, u32[]{:S(2)}) collective-permute-start(bf16[128,1152]{1,0:T(8,128)(2,1)S(1)} %copy.11), channel_id=1, source_target_pairs={{0,767},{1,0},{2,1},{3,2},{4,3},{5,4},{6,5},{7,6},{8,7},{9,8},{10,... | collective-permute-start | bytes 884744 | tf_op jit(solution)/shard_map/while/body/eval_jaxpr/ppermute | solution.py:14
where the time goes:
time: 375 us; the launch traced here: 373 us
  waiting for transfers between devices  173 us (46%)
  starting transfers between devices  143 us (38%)
  matrix products  26.5 us (7%)
  loops' own time  13.4 us (4%)
  local copies, waits for them, and re-layouts  12.1 us (3%)
    ppermute x38, waiting for transfers between devices, shifted(): return lax.ppermute(value, axis, pairs)  173 us
    ppermute x38, starting transfers between devices, shifted(): return lax.ppermute(value, axis, pairs)  143 us
    dot_general x20, matrix products, text_terms(): lax.dot_general(weights, image_block, (((0,), (0,)), ((), ())), preferred...  14.1 us
    another operation x1, loops' own time, per_device(): lax.scan(advance, (text_low, image_reduced, zeros, zeros), jnp.arange(win...  13.4 us
    dot_general x19, matrix products, advance(): jnp.dot(weights, text_block, preferred_element_type=jnp.float32)  11.8 us
    dynamic_slice x19, local copies, waits for them, and re-layouts, per_device(): lax.scan(advance, (text_low, image_reduced, zeros, zeros), jnp.arange(win...  11.1 us
  transfers between devices with their start and end apart: 38, of which 38 were waited for; matrix products, arithmetic and copies ran while one was open for 10% of the time, Pallas kernels for 0%

commit v1 on v0

v1 whole, which is shorter than its diff:
```python
import jax
import jax.numpy as jnp
from jax import lax
from jax.experimental import pallas as pl
from jax.experimental.pallas import tpu as pltpu
from jax.sharding import PartitionSpec as P

MESH = pl.DeviceIdType.MESH
LOGIT_SCALE = 10.0
BIAS_LOGIT = -2.0
EPSILON = 1e-06
ROWS = 128
WIDTH = 1152
CHUNKS = 2
PIECE = ROWS // CHUNKS
COLS = 384
F32 = jnp.float32
BF16 = jnp.bfloat16


def unit_and_inverse(ref):
    wide = ref[...].astype(F32)
    length = jnp.sqrt(jnp.sum(wide * wide, axis=-1, keepdims=True) + EPSILON)
    inverse = 1.0 / length
    return wide * inverse, inverse


def undo(total, ref):
    unit, inverse = unit_and_inverse(ref)
    grad = LOGIT_SCALE * total
    inner = jnp.sum(unit * grad, axis=-1, keepdims=True)
    return ((grad - unit * inner) * inverse).astype(BF16)


def kernel(
    blocks,
    image_ref, text_ref, image_out, text_out,
    img, txt, wgt, q_sum, p_sum,
    q_send, q_recv, far_out, near_out, near_in, far_in, p_send, p_recv,
    txt_ssem, txt_rsem, img_fsem, img_nsem, img_psem, img_rsem,
    q_ssem, q_rsem, far_ssem, near_ssem, near_rsem, far_rsem, p_ssem, p_rsem,
):
    blk = lax.axis_index("blk")
    z = lax.axis_index("grp")
    k = lax.rem(blk, 2)
    j = 4 * k + z
    high = z // 2
    sign = 1 - 2 * high
    middle = (z == 1) | (z == 2)
    edge = (z == 0) | (z == 3)

    def spot(t):
        return 3 * high + sign * t

    partner = (blk + 1 - 2 * k, z)
    ahead = (lax.rem(blk + 2, blocks), z)
    behind = (lax.rem(blk + blocks - 2, blocks), z)
    far = (blk, z + sign)
    near = (blk, z - sign)

    def copy(src, dst, ssem, rsem, device):
        return pltpu.make_async_remote_copy(
            src_ref=src, dst_ref=dst, send_sem=ssem, recv_sem=rsem, device_id=device, device_id_type=MESH
        )

    def rows(h):
        return pl.ds(h * PIECE, PIECE)

    barrier = pltpu.get_barrier_semaphore()
    for device in (partner, ahead, behind, far):
        pl.semaphore_signal(barrier, inc=1, device_id=device, device_id_type=MESH)

    @pl.when(middle)
    def _():
        pl.semaphore_signal(barrier, inc=1, device_id=near, device_id_type=MESH)

    unit, _ = unit_and_inverse(image_ref)
    img[k, z] = unit.astype(BF16)
    unit, _ = unit_and_inverse(text_ref)
    txt[0] = unit.astype(BF16)

    pl.semaphore_wait(barrier, 4 + z * (3 - z) // 2)

    def image_copy(t, h, ssem, device):
        s = spot(t)
        ref = img.at[k, s, rows(h)]
        return copy(ref, ref, ssem.at[t, h], img_rsem.at[k, s, h], device)

    def image_arrival(kk, s, h):
        ref = img.at[kk, s, rows(h)]
        copy(ref, ref, img_psem.at[0, h], img_rsem.at[kk, s, h], partner).wait_recv()

    def text_copy(d, h):
        return copy(
            txt.at[d, rows(h)], txt.at[d + 1, rows(h)], txt_ssem.at[d, h], txt_rsem.at[d, h], ahead
        )

    def text_arrival(d, h):
        copy(
            txt.at[d, rows(h)], txt.at[d + 1, rows(h)], txt_ssem.at[d, h], txt_rsem.at[d, h], ahead
        ).wait_recv()

    for h in range(CHUNKS):
        text_copy(0, h).start()

        @pl.when(edge)
        def _():
            image_copy(0, h, img_fsem, far).start()
            image_copy(0, h, img_psem, partner).start()

        @pl.when(middle)
        def _():
            image_copy(1, h, img_fsem, far).start()
            image_copy(1, h, img_nsem, near).start()
            image_copy(1, h, img_psem, partner).start()

    for u in range(3):
        for h in range(CHUNKS):
            @pl.when(edge)
            def _():
                image_arrival(k, spot(u + 1), h)
                image_copy(u + 1, h, img_psem, partner).start()

            @pl.when(middle)
            def _():
                if u == 0:
                    image_arrival(k, spot(0), h)
                    image_copy(0, h, img_fsem, far).start()
                    image_copy(0, h, img_psem, partner).start()
                else:
                    image_arrival(k, spot(u + 1), h)
                    image_copy(u + 1, h, img_nsem, near).start()
                    image_copy(u + 1, h, img_psem, partner).start()

            if u < 2:
                text_arrival(u, h)
                if u == 0:
                    text_copy(1, h).start()
                else:
                    @pl.when(j >= 5)
                    def _():
                        text_copy(2, h).start()
            else:
                @pl.when(j >= 5)
                def _():
                    text_arrival(2, h)

    @pl.when(j < 5)
    def _():
        txt[3] = jnp.zeros((ROWS, WIDTH), BF16)

    for s in range(4):
        for h in range(CHUNKS):
            image_arrival(1 - k, s, h)

    p_sum[...] = jnp.zeros_like(p_sum)

    @pl.loop(0, 4)
    def _(s):
        pair = img[:, s].reshape(2 * ROWS, WIDTH)
        texts = txt[...].reshape(4 * ROWS, WIDTH)
        logits = (
            LOGIT_SCALE
            * lax.dot_general(pair, texts, (((1,), (1,)), ((), ())), preferred_element_type=F32)
            + BIAS_LOGIT
        )
        row = lax.broadcasted_iota(jnp.int32, logits.shape, 0)
        col = lax.broadcasted_iota(jnp.int32, logits.shape, 1)
        gap = 8 * (col // ROWS) + 4 * (row // ROWS) + (s - j)
        match = (gap == 0) & (lax.rem(row, ROWS) == lax.rem(col, ROWS))
        weight = jax.nn.sigmoid(jnp.where(match, -logits, logits))
        weight = jnp.where(match, -weight, weight)
        weight = jnp.where((gap >= 0) & (gap <= 19), weight, 0.0)
        wgt[...] = weight.astype(BF16)
        for n in range(WIDTH // COLS):
            part = pl.ds(n * COLS, COLS)
            texts = txt[:, :, part].reshape(4 * ROWS, COLS)
            q = jnp.dot(wgt[...], texts, preferred_element_type=F32)
            q_sum[:, s, :, part] = q.reshape(2, ROWS, COLS)
            pair = img[:, s, :, part].reshape(2 * ROWS, COLS)
            p = lax.dot_general(wgt[...], pair, (((0,), (0,)), ((), ())), preferred_element_type=F32)
            p_sum[:, :, part] += p.reshape(4, ROWS, COLS)
        q_send[s] = q_sum[1 - k, s].astype(BF16)
        copy(q_send.at[s], q_recv.at[s], q_ssem.at[s], q_rsem.at[s], partner).start()

    def back_copy(d, h):
        return copy(p_send.at[d, rows(h)], p_recv.at[d, rows(h)], p_ssem.at[d, h], p_rsem.at[d, h], behind)

    def far_copy(t, h, receiver):
        s = spot(t)
        sem = {"near": near_rsem, "far": far_rsem}[receiver]
        dst = {"near": near_in, "far": far_in}[receiver]
        return copy(far_out.at[s, rows(h)], dst.at[s, rows(h)], far_ssem.at[s, h], sem.at[s, h], far)

    def near_copy(h):
        s = spot(0)
        return copy(near_out.at[rows(h)], far_in.at[s, rows(h)], near_ssem.at[h], far_rsem.at[s, h], near)

    def near_arrival(t, h):
        s = spot(t)
        copy(far_out.at[s, rows(h)], near_in.at[s, rows(h)], far_ssem.at[s, h], near_rsem.at[s, h], far).wait_recv()

    def far_arrival(t, h):
        s = spot(t)
        copy(far_out.at[s, rows(h)], far_in.at[s, rows(h)], far_ssem.at[s, h], far_rsem.at[s, h], far).wait_recv()

    @pl.when(j >= 5)
    def _():
        p_send[2] = p_sum[3].astype(BF16)
        for h in range(CHUNKS):
            back_copy(2, h).start()

    @pl.loop(0, 4)
    def _(s):
        copy(q_send.at[s], q_recv.at[s], q_ssem.at[s], q_rsem.at[s], partner).wait_recv()

    for u in range(3):
        for h in range(CHUNKS):
            r = rows(h)

            @pl.when(edge)
            def _():
                t = spot(3 - u)
                far_out[t, r] = (q_sum[k, t, r] + q_recv[t, r].astype(F32)).astype(BF16)
                far_copy(3 - u, h, "near").start()

            if u < 2:
                @pl.when(middle)
                def _():
                    t = spot(3 - u)
                    near_arrival(3 - u, h)
                    total = q_sum[k, t, r] + q_recv[t, r].astype(F32) + near_in[t, r].astype(F32)
                    far_out[t, r] = total.astype(BF16)
                    far_copy(3 - u, h, "far").start()

            if u == 1:
                @pl.when(middle)
                def _():
                    t = spot(0)
                    far_arrival(0, h)
                    total = q_sum[k, t, r] + q_recv[t, r].astype(F32) + far_in[t, r].astype(F32)
                    near_out[r] = total.astype(BF16)
                    near_copy(h).start()

            if u == 0:
                @pl.when(j >= 5)
                def _():
                    copy(p_send.at[2, r], p_recv.at[2, r], p_ssem.at[2, h], p_rsem.at[2, h], behind).wait_recv()
                    p_send[1, r] = (p_sum[2, r] + p_recv[2, r].astype(F32)).astype(BF16)
                    back_copy(1, h).start()

                @pl.when(j < 5)
                def _():
                    p_send[1, r] = p_sum[2, r].astype(BF16)
                    back_copy(1, h).start()

            if u == 1:
                copy(p_send.at[1, r], p_recv.at[1, r], p_ssem.at[1, h], p_rsem.at[1, h], behind).wait_recv()
                p_send[0, r] = (p_sum[1, r] + p_recv[1, r].astype(F32)).astype(BF16)
                back_copy(0, h).start()

    for h in range(CHUNKS):
        r = rows(h)
        copy(p_send.at[0, r], p_recv.at[0, r], p_ssem.at[0, h], p_rsem.at[0, h], behind).wait_recv()
    text_out[...] = undo(p_sum[0] + p_recv[0].astype(F32), text_ref)

    @pl.when(edge)
    def _():
        for h in range(CHUNKS):
            far_arrival(0, h)
        total = q_sum[k, z] + q_recv[z].astype(F32) + far_in[z].astype(F32)
        image_out[...] = undo(total, image_ref)

    @pl.when(middle)
    def _():
        for h in range(CHUNKS):
            near_arrival(1, h)
            far_arrival(1, h)
        total = q_sum[k, z] + q_recv[z].astype(F32) + near_in[z].astype(F32) + far_in[z].astype(F32)
        image_out[...] = undo(total, image_ref)

    for h in range(CHUNKS):
        text_copy(0, h).wait_send()
        text_copy(1, h).wait_send()
        back_copy(0, h).wait_send()
        back_copy(1, h).wait_send()

        @pl.when(j >= 5)
        def _():
            text_copy(2, h).wait_send()
            back_copy(2, h).wait_send()

        for t in range(4):
            image_copy(t, h, img_psem, partner).wait_send()

        @pl.when(edge)
        def _():
            image_copy(0, h, img_fsem, far).wait_send()
            for t in (1, 2, 3):
                far_copy(t, h, "near").wait_send()

        @pl.when(middle)
        def _():
            for t in (0, 1):
                image_copy(t, h, img_fsem, far).wait_send()
            for t in (1, 2, 3):
                image_copy(t, h, img_nsem, near).wait_send()
            for t in (2, 3):
                far_copy(t, h, "far").wait_send()
            near_copy(h).wait_send()

    @pl.loop(0, 4)
    def _(s):
        copy(q_send.at[s], q_recv.at[s], q_ssem.at[s], q_rsem.at[s], partner).wait_send()


def solution(mesh):
    blocks = mesh.shape["blk"]
    dma = pltpu.SemaphoreType.DMA
    block = (ROWS, WIDTH)

    def per_device(image_embeds, text_embeds):
        out = jax.ShapeDtypeStruct(block, BF16)
        vmem = pl.BlockSpec(memory_space=pltpu.VMEM)
        return pl.pallas_call(
            lambda *refs: kernel(blocks, *refs),
            out_shape=(out, out),
            in_specs=[vmem, vmem],
            out_specs=(vmem, vmem),
            scratch_shapes=[
                pltpu.VMEM((2, 4) + block, BF16),
                pltpu.VMEM((4,) + block, BF16),
                pltpu.VMEM((2 * ROWS, 4 * ROWS), BF16),
                pltpu.VMEM((2, 4) + block, F32),
                pltpu.VMEM((4,) + block, F32),
                pltpu.VMEM((4,) + block, BF16),
                pltpu.VMEM((4,) + block, BF16),
                pltpu.VMEM((4,) + block, BF16),
                pltpu.VMEM(block, BF16),
                pltpu.VMEM((4,) + block, BF16),
                pltpu.VMEM((4,) + block, BF16),
                pltpu.VMEM((3,) + block, BF16),
                pltpu.VMEM((3,) + block, BF16),
                dma((3, CHUNKS)),
                dma((3, CHUNKS)),
                dma((4, CHUNKS)),
                dma((4, CHUNKS)),
                dma((4, CHUNKS)),
                dma((2, 4, CHUNKS)),
                dma((4,)),
                dma((4,)),
                dma((4, CHUNKS)),
                dma((CHUNKS,)),
                dma((4, CHUNKS)),
                dma((4, CHUNKS)),
                dma((3, CHUNKS)),
                dma((3, CHUNKS)),
            ],
            compiler_params=pltpu.CompilerParams(
                collective_id=0, has_side_effects=True, vmem_limit_bytes=56 * 1024 * 1024
            ),
            name="pair_window",
        )(image_embeds, text_embeds)

    spec = P(("blk", "grp"), None)
    return jax.shard_map(
        per_device, mesh=mesh, in_specs=(spec, spec), out_specs=(spec, spec), check_vma=False
    )
```

time: 375 us -> 183 us (0.49)
  the two profiles are of different devices: /device:TPU:1 before, /device:TPU:129 now
where the time goes in v1:
time: 183 us
  Pallas kernels  180 us (98%)
  local copies, waits for them, and re-layouts  2.46 us (1%)
    pallas_call x1, Pallas kernels, per_device(): pl.pallas_call(lambda *refs: kernel(blocks, *refs), out_shape=(out, out),...  180 us

profile of v1, /device:TPU:129, one launch (start us, length us, event | category | flops | bytes accessed | tf_op | source)
XLA Modules:
  0.0 183.3 jit_solution(13435332043137786755)
XLA Ops:
  0.6 180.2 %pair_window.1 = (bf16[128,1152]{1,0:T(8,128)(2,1)}, bf16[128,1152]{1,0:T(8,128)(2,1)}) custom-call(bf16[128,1152]{1,0:T(8,128)(2,1)} %refs_0_.1, bf16[128,1152]{1,0:T(8,128)(2,1)} %refs_1_.1), custom_call_target="tpu_custom_call" | custom-call | tf_op jit(solution)/shard_map/pair_window/pallas_call | solution.py:325
  180.9 0.0 copy-start
  180.9 1.7 copy.6
  182.6 0.0 copy-done
  182.6 0.7 copy.7
Async XLA Ops:
  180.9 1.8 copy-start

commit v2 on v1

--- a/solution.py
+++ b/solution.py
@@ -13,6 +13,9 @@
 WIDTH = 1152
 CHUNKS = 2
 PIECE = ROWS // CHUNKS
+SLICES = 4
+THIN = ROWS // SLICES
+RELAYS = ((24, 7, 1, 30), (23, 8, 15, 16))
 COLS = 384
 F32 = jnp.float32
 BF16 = jnp.bfloat16
@@ -37,8 +40,10 @@
     image_ref, text_ref, image_out, text_out,
     img, txt, wgt, q_sum, p_sum,
     q_send, q_recv, far_out, near_out, near_in, far_in, p_send, p_recv,
+    fwd_hold, back_hold,
     txt_ssem, txt_rsem, img_fsem, img_nsem, img_psem, img_rsem,
     q_ssem, q_rsem, far_ssem, near_ssem, near_rsem, far_rsem, p_ssem, p_rsem,
+    fwd_ssem, fwd_rsem, back_ssem, back_rsem,
 ):
     blk = lax.axis_index("blk")
     z = lax.axis_index("grp")
@@ -52,6 +57,24 @@
     def spot(t):
         return 3 * high + sign * t
 
+    column = blk // 2
+    third = column // 32
+    place = lax.rem(column, 32)
+    first = place == 0
+    last = place == 31
+
+    def relay_place(h):
+        return RELAYS[0][h] + k * (RELAYS[1][h] - RELAYS[0][h])
+
+    def at(hop, where):
+        return (2 * (32 * lax.rem(third + hop, blocks // 64) + where) + k, z)
+
+    is_role = [jnp.where(place == relay_place(h), 1, 0) for h in range(SLICES)]
+    role = is_role[1] + 2 * is_role[2] + 3 * is_role[3]
+    relay = is_role[0] + is_role[1] + is_role[2] + is_role[3] > 0
+    next_first, own_first = at(1, 0), at(0, 0)
+    prev_last, own_last = at(blocks // 64 - 1, 31), at(0, 31)
+
     partner = (blk + 1 - 2 * k, z)
     ahead = (lax.rem(blk + 2, blocks), z)
     behind = (lax.rem(blk + blocks - 2, blocks), z)
@@ -66,6 +89,9 @@
     def rows(h):
         return pl.ds(h * PIECE, PIECE)
 
+    def thin(h):
+        return pl.ds(pl.multiple_of(h * THIN, THIN), THIN)
+
     barrier = pltpu.get_barrier_semaphore()
     for device in (partner, ahead, behind, far):
         pl.semaphore_signal(barrier, inc=1, device_id=device, device_id_type=MESH)
@@ -73,13 +99,31 @@
     @pl.when(middle)
     def _():
         pl.semaphore_signal(barrier, inc=1, device_id=near, device_id_type=MESH)
+
+    @pl.when(relay)
+    def _():
+        for device in (next_first, own_first, prev_last, own_last):
+            pl.semaphore_signal(barrier, inc=1, device_id=device, device_id_type=MESH)
+
+    @pl.when(first)
+    def _():
+        for h in range(SLICES):
+            for device in (at(0, relay_place(h)), at(blocks // 64 - 1, relay_place(h))):
+                pl.semaphore_signal(barrier, inc=1, device_id=device, device_id_type=MESH)
+
+    @pl.when(last)
+    def _():
+        for h in range(SLICES):
+            for device in (at(0, relay_place(h)), at(1, relay_place(h))):
+                pl.semaphore_signal(barrier, inc=1, device_id=device, device_id_type=MESH)
 
     unit, _ = unit_and_inverse(image_ref)
     img[k, z] = unit.astype(BF16)
     unit, _ = unit_and_inverse(text_ref)
     txt[0] = unit.astype(BF16)
 
-    pl.semaphore_wait(barrier, 4 + z * (3 - z) // 2)
+    greeted = 4 + z * (3 - z) // 2 + jnp.where(relay, 4, 0) + jnp.where(first | last, 2 * SLICES, 0)
+    pl.semaphore_wait(barrier, greeted)
 
     def image_copy(t, h, ssem, device):
         s = spot(t)
@@ -92,17 +136,35 @@
 
     def text_copy(d, h):
         return copy(
-            txt.at[d, rows(h)], txt.at[d + 1, rows(h)], txt_ssem.at[d, h], txt_rsem.at[d, h], ahead
+            txt.at[d, thin(h)], txt.at[d + 1, thin(h)], txt_ssem.at[d, h], txt_rsem.at[d, h], ahead
         )
 
-    def text_arrival(d, h):
-        copy(
-            txt.at[d, rows(h)], txt.at[d + 1, rows(h)], txt_ssem.at[d, h], txt_rsem.at[d, h], ahead
-        ).wait_recv()
+    def text_start(d, h):
+        @pl.when(last)
+        def _():
+            copy(
+                txt.at[d, thin(h)], fwd_hold.at[d], txt_ssem.at[d, h], fwd_rsem.at[d], at(0, relay_place(h))
+            ).start()
+
+        @pl.when(jnp.logical_not(last))
+        def _():
+            text_copy(d, h).start()
+
+    def text_relay(d):
+        return copy(
+            fwd_hold.at[d], txt.at[d + 1, thin(role)], fwd_ssem.at[d], txt_rsem.at[d, role], next_first
+        )
+
+    def text_relay_stage(d):
+        @pl.when(relay & (j >= 5) if d == 2 else relay)
+        def _():
+            copy(fwd_hold.at[d], fwd_hold.at[d], fwd_ssem.at[d], fwd_rsem.at[d], next_first).wait_recv()
+            text_relay(d).start()
+
+    for h in range(SLICES):
+        text_start(0, h)
 
     for h in range(CHUNKS):
-        text_copy(0, h).start()
-
         @pl.when(edge)
         def _():
             image_copy(0, h, img_fsem, far).start()
@@ -115,6 +177,7 @@
             image_copy(1, h, img_psem, partner).start()
 
     for u in range(3):
+        text_relay_stage(u)
         for h in range(CHUNKS):
             @pl.when(edge)
             def _():
@@ -132,18 +195,20 @@
                     image_copy(u + 1, h, img_nsem, near).start()
                     image_copy(u + 1, h, img_psem, partner).start()
 
-            if u < 2:
-                text_arrival(u, h)
+        if u < 2:
+            for h in range(SLICES):
+                text_copy(u, h).wait_recv()
                 if u == 0:
-                    text_copy(1, h).start()
+                    text_start(1, h)
                 else:
                     @pl.when(j >= 5)
                     def _():
-                        text_copy(2, h).start()
-            else:
-                @pl.when(j >= 5)
-                def _():
-                    text_arrival(2, h)
+                        text_start(2, h)
+        else:
+            @pl.when(j >= 5)
+            def _():
+                for h in range(SLICES):
+                    text_copy(2, h).wait_recv()
 
     @pl.when(j < 5)
     def _():
@@ -184,7 +249,29 @@
         copy(q_send.at[s], q_recv.at[s], q_ssem.at[s], q_rsem.at[s], partner).start()
 
     def back_copy(d, h):
-        return copy(p_send.at[d, rows(h)], p_recv.at[d, rows(h)], p_ssem.at[d, h], p_rsem.at[d, h], behind)
+        return copy(p_send.at[d, thin(h)], p_recv.at[d, thin(h)], p_ssem.at[d, h], p_rsem.at[d, h], behind)
+
+    def back_start(d, h):
+        @pl.when(first)
+        def _():
+            copy(
+                p_send.at[d, thin(h)], back_hold.at[d], p_ssem.at[d, h], back_rsem.at[d], at(0, relay_place(h))
+            ).start()
+
+        @pl.when(jnp.logical_not(first))
+        def _():
+            back_copy(d, h).start()
+
+    def back_relay(d):
+        return copy(
+            back_hold.at[d], p_recv.at[d, thin(role)], back_ssem.at[d], p_rsem.at[d, role], prev_last
+        )
+
+    def back_relay_stage(d):
+        @pl.when(relay & (j >= 5) if d == 2 else relay)
+        def _():
+            copy(back_hold.at[d], back_hold.at[d], back_ssem.at[d], back_rsem.at[d], prev_last).wait_recv()
+            back_relay(d).start()
 
     def far_copy(t, h, receiver):
         s = spot(t)
@@ -207,8 +294,8 @@
     @pl.when(j >= 5)
     def _():
         p_send[2] = p_sum[3].astype(BF16)
-        for h in range(CHUNKS):
-            back_copy(2, h).start()
+        for h in range(SLICES):
+            back_start(2, h)
 
     @pl.loop(0, 4)
     def _(s):
@@ -242,26 +329,28 @@
                     near_out[r] = total.astype(BF16)
                     near_copy(h).start()
 
-            if u == 0:
-                @pl.when(j >= 5)
-                def _():
-                    copy(p_send.at[2, r], p_recv.at[2, r], p_ssem.at[2, h], p_rsem.at[2, h], behind).wait_recv()
-                    p_send[1, r] = (p_sum[2, r] + p_recv[2, r].astype(F32)).astype(BF16)
-                    back_copy(1, h).start()
-
-                @pl.when(j < 5)
-                def _():
-                    p_send[1, r] = p_sum[2, r].astype(BF16)
-                    back_copy(1, h).start()
-
-            if u == 1:
-                copy(p_send.at[1, r], p_recv.at[1, r], p_ssem.at[1, h], p_rsem.at[1, h], behind).wait_recv()
-                p_send[0, r] = (p_sum[1, r] + p_recv[1, r].astype(F32)).astype(BF16)
-                back_copy(0, h).start()
-
-    for h in range(CHUNKS):
-        r = rows(h)
-        copy(p_send.at[0, r], p_recv.at[0, r], p_ssem.at[0, h], p_rsem.at[0, h], behind).wait_recv()
+        back_relay_stage(2 - u)
+        if u < 2:
+            for h in range(SLICES):
+                r = thin(h)
+                if u == 0:
+                    @pl.when(j >= 5)
+                    def _():
+                        back_copy(2, h).wait_recv()
+                        p_send[1, r] = (p_sum[2, r] + p_recv[2, r].astype(F32)).astype(BF16)
+                        back_start(1, h)
+
+                    @pl.when(j < 5)
+                    def _():
+                        p_send[1, r] = p_sum[2, r].astype(BF16)
+                        back_start(1, h)
+                else:
+                    back_copy(1, h).wait_recv()
+                    p_send[0, r] = (p_sum[1, r] + p_recv[1, r].astype(F32)).astype(BF16)
+                    back_start(0, h)
+
+    for h in range(SLICES):
+        back_copy(0, h).wait_recv()
     text_out[...] = undo(p_sum[0] + p_recv[0].astype(F32), text_ref)
 
     @pl.when(edge)
@@ -279,17 +368,19 @@
         total = q_sum[k, z] + q_recv[z].astype(F32) + near_in[z].astype(F32) + far_in[z].astype(F32)
         image_out[...] = undo(total, image_ref)
 
+    for d in range(3):
+        @pl.when(relay & (j >= 5) if d == 2 else relay)
+        def _():
+            text_relay(d).wait_send()
+            back_relay(d).wait_send()
+
+        @pl.when(j >= (5 if d == 2 else 0))
+        def _():
+            for h in range(SLICES):
+                text_copy(d, h).wait_send()
+                back_copy(d, h).wait_send()
+
     for h in range(CHUNKS):
-        text_copy(0, h).wait_send()
-        text_copy(1, h).wait_send()
-        back_copy(0, h).wait_send()
-        back_copy(1, h).wait_send()
-
-        @pl.when(j >= 5)
-        def _():
-            text_copy(2, h).wait_send()
-            back_copy(2, h).wait_send()
-
         for t in range(4):
             image_copy(t, h, img_psem, partner).wait_send()
 
@@ -341,8 +432,10 @@
                 pltpu.VMEM((4,) + block, BF16),
                 pltpu.VMEM((3,) + block, BF16),
                 pltpu.VMEM((3,) + block, BF16),
-                dma((3, CHUNKS)),
-                dma((3, CHUNKS)),
+                pltpu.VMEM((3, THIN, WIDTH), BF16),
+                pltpu.VMEM((3, THIN, WIDTH), BF16),
+                dma((3, SLICES)),
+                dma((3, SLICES)),
                 dma((4, CHUNKS)),
                 dma((4, CHUNKS)),
                 dma((4, CHUNKS)),
@@ -353,8 +446,12 @@
                 dma((CHUNKS,)),
                 dma((4, CHUNKS)),
                 dma((4, CHUNKS)),
-                dma((3, CHUNKS)),
-                dma((3, CHUNKS)),
+                dma((3, SLICES)),
+                dma((3, SLICES)),
+                dma((3,)),
+                dma((3,)),
+                dma((3,)),
+                dma((3,)),
             ],
             compiler_params=pltpu.CompilerParams(
                 collective_id=0, has_side_effects=True, vmem_limit_bytes=56 * 1024 * 1024

time: 183 us -> 93.4 us (0.51)
  the two profiles are of different devices: /device:TPU:129 before, /device:TPU:182 now
where the time goes in v2:
time: 93.4 us; the launch traced here: 93.3 us
  Pallas kernels  90.2 us (97%)
  local copies, waits for them, and re-layouts  2.46 us (3%)
    pallas_call x1, Pallas kernels, per_device(): pl.pallas_call(lambda *refs: kernel(blocks, *refs), out_shape=(out, out),...  90.2 us
    unnamed x4, local copies, waits for them, and re-layouts  2.46 us

profile of v2, /device:TPU:182, one launch (start us, length us, event | category | flops | bytes accessed | tf_op | source)
XLA Modules:
  0.0 93.3 jit_solution(10057752584605468682)
XLA Ops:
  0.6 90.2 %pair_window.1 = (bf16[128,1152]{1,0:T(8,128)(2,1)}, bf16[128,1152]{1,0:T(8,128)(2,1)}) custom-call(bf16[128,1152]{1,0:T(8,128)(2,1)} %refs_0_.1, bf16[128,1152]{1,0:T(8,128)(2,1)} %refs_1_.1), custom_call_target="tpu_custom_call" | custom-call | tf_op jit(solution)/shard_map/pair_window/pallas_call | solution.py:416
  90.8 0.0 copy-start
  90.8 1.7 %copy.6 = bf16[128,1152]{1,0:T(8,128)(2,1)} copy(bf16[128,1152]{1,0:T(8,128)(2,1)} %get-tuple-element.4) | data formatting | bytes 589824
  92.5 0.0 copy-done
  92.5 0.7 copy.7
Async XLA Ops:
  90.8 1.8 %copy-start = (bf16[128,1152]{1,0:T(8,128)(2,1)S(1)}, bf16[128,1152]{1,0:T(8,128)(2,1)}, u32[]{:S(2)}) copy-start(bf16[128,1152]{1,0:T(8,128)(2,1)} %get-tuple-element.5) | copy-start | bytes 884740

commit v3 on v2

--- a/solution.py
+++ b/solution.py
@@ -15,7 +15,7 @@
 PIECE = ROWS // CHUNKS
 SLICES = 4
 THIN = ROWS // SLICES
-RELAYS = ((24, 7, 1, 30), (23, 8, 15, 16))
+RELAYS = ((24, 7, 1, 30), (23, 8, 15, 6))
 COLS = 384
 F32 = jnp.float32
 BF16 = jnp.bfloat16
@@ -69,9 +69,11 @@
     def at(hop, where):
         return (2 * (32 * lax.rem(third + hop, blocks // 64) + where) + k, z)
 
-    is_role = [jnp.where(place == relay_place(h), 1, 0) for h in range(SLICES)]
-    role = is_role[1] + 2 * is_role[2] + 3 * is_role[3]
-    relay = is_role[0] + is_role[1] + is_role[2] + is_role[3] > 0
+    role, relay = 0, False
+    for h in range(SLICES):
+        match = place == relay_place(h)
+        role = role + jnp.where(match, h, 0)
+        relay = relay | match
     next_first, own_first = at(1, 0), at(0, 0)
     prev_last, own_last = at(blocks // 64 - 1, 31), at(0, 31)
 
@@ -93,36 +95,28 @@
         return pl.ds(pl.multiple_of(h * THIN, THIN), THIN)
 
     barrier = pltpu.get_barrier_semaphore()
-    for device in (partner, ahead, behind, far):
+
+    def greet(condition, devices):
+        @pl.when(condition)
+        def _():
+            for device in devices:
+                pl.semaphore_signal(barrier, inc=1, device_id=device, device_id_type=MESH)
+
+    greet(relay, (own_last, own_first))
+    greet(first, [at(blocks // 64 - 1, relay_place(h)) for h in range(SLICES)])
+    greet(last, [at(1, relay_place(h)) for h in range(SLICES)])
+    for device in (partner, far):
         pl.semaphore_signal(barrier, inc=1, device_id=device, device_id_type=MESH)
-
-    @pl.when(middle)
-    def _():
-        pl.semaphore_signal(barrier, inc=1, device_id=near, device_id_type=MESH)
-
-    @pl.when(relay)
-    def _():
-        for device in (next_first, own_first, prev_last, own_last):
-            pl.semaphore_signal(barrier, inc=1, device_id=device, device_id_type=MESH)
-
-    @pl.when(first)
-    def _():
-        for h in range(SLICES):
-            for device in (at(0, relay_place(h)), at(blocks // 64 - 1, relay_place(h))):
-                pl.semaphore_signal(barrier, inc=1, device_id=device, device_id_type=MESH)
-
-    @pl.when(last)
-    def _():
-        for h in range(SLICES):
-            for device in (at(0, relay_place(h)), at(1, relay_place(h))):
-                pl.semaphore_signal(barrier, inc=1, device_id=device, device_id_type=MESH)
+    greet(middle, (near,))
+    greet(jnp.logical_not(first), (behind,))
+    greet(jnp.logical_not(last), (ahead,))
 
     unit, _ = unit_and_inverse(image_ref)
     img[k, z] = unit.astype(BF16)
     unit, _ = unit_and_inverse(text_ref)
     txt[0] = unit.astype(BF16)
 
-    greeted = 4 + z * (3 - z) // 2 + jnp.where(relay, 4, 0) + jnp.where(first | last, 2 * SLICES, 0)
+    greeted = 4 + z * (3 - z) // 2 + jnp.where(relay, 2, 0) + jnp.where(first | last, SLICES - 1, 0)
     pl.semaphore_wait(barrier, greeted)
 
     def image_copy(t, h, ssem, device):
@@ -164,7 +158,94 @@
     for h in range(SLICES):
         text_start(0, h)
 
-    for h in range(CHUNKS):
+    def back_copy(d, h):
+        return copy(p_send.at[d, thin(h)], p_recv.at[d, thin(h)], p_ssem.at[d, h], p_rsem.at[d, h], behind)
+
+    def back_start(d, h):
+        @pl.when(first)
+        def _():
+            copy(
+                p_send.at[d, thin(h)], back_hold.at[d], p_ssem.at[d, h], back_rsem.at[d], at(0, relay_place(h))
+            ).start()
+
+        @pl.when(jnp.logical_not(first))
+        def _():
+            back_copy(d, h).start()
+
+    def back_relay(d):
+        return copy(
+            back_hold.at[d], p_recv.at[d, thin(role)], back_ssem.at[d], p_rsem.at[d, role], prev_last
+        )
+
+    def back_relay_stage(d):
+        copy(back_hold.at[d], back_hold.at[d], back_ssem.at[d], back_rsem.at[d], prev_last).wait_recv()
+        back_relay(d).start()
+
+    def far_copy(t, h, receiver):
+        s = spot(t)
+        sem = {"near": near_rsem, "far": far_rsem}[receiver]
+        dst = {"near": near_in, "far": far_in}[receiver]
+        return copy(far_out.at[s, rows(h)], dst.at[s, rows(h)], far_ssem.at[s, h], sem.at[s, h], far)
+
+    def near_copy(h):
+        s = spot(0)
+        return copy(near_out.at[rows(h)], far_in.at[s, rows(h)], near_ssem.at[h], far_rsem.at[s, h], near)
+
+    def near_arrival(t, h):
+        s = spot(t)
+        copy(far_out.at[s, rows(h)], near_in.at[s, rows(h)], far_ssem.at[s, h], near_rsem.at[s, h], far).wait_recv()
+
+    def far_arrival(t, h):
+        s = spot(t)
+        copy(far_out.at[s, rows(h)], far_in.at[s, rows(h)], far_ssem.at[s, h], far_rsem.at[s, h], far).wait_recv()
+
+    def sum_arrival(t):
+        s = spot(t)
+        copy(q_send.at[s], q_recv.at[s], q_ssem.at[s], q_rsem.at[s], partner).wait_recv()
+
+    def own_part(s, r):
+        return q_sum[k, s, r] + q_recv[s, r].astype(F32)
+
+    def far_start(t):
+        sum_arrival(t)
+        s = spot(t)
+        for h in range(CHUNKS):
+            r = rows(h)
+            far_out[s, r] = own_part(s, r).astype(BF16)
+            far_copy(t, h, "near").start()
+
+    def far_pass(t):
+        sum_arrival(t)
+        s = spot(t)
+        for h in range(CHUNKS):
+            r = rows(h)
+            near_arrival(t, h)
+            far_out[s, r] = (own_part(s, r) + near_in[s, r].astype(F32)).astype(BF16)
+            far_copy(t, h, "far").start()
+
+    def near_pass():
+        sum_arrival(0)
+        s = spot(0)
+        for h in range(CHUNKS):
+            r = rows(h)
+            far_arrival(0, h)
+            near_out[r] = (own_part(s, r) + far_in[s, r].astype(F32)).astype(BF16)
+            near_copy(h).start()
+
+    def back_begin(d):
+        for h in range(SLICES):
+            r = thin(h)
+            p_send[d - 1, r] = p_sum[d, r].astype(BF16)
+            back_start(d - 1, h)
+
+    def back_pass(d):
+        for h in range(SLICES):
+            r = thin(h)
+            back_copy(d, h).wait_recv()
+            p_send[d - 1, r] = (p_sum[d, r] + p_recv[d, r].astype(F32)).astype(BF16)
+            back_start(d - 1, h)
+
+    def image_first(h):
         @pl.when(edge)
         def _():
             image_copy(0, h, img_fsem, far).start()
@@ -176,8 +257,7 @@
             image_copy(1, h, img_nsem, near).start()
             image_copy(1, h, img_psem, partner).start()
 
-    for u in range(3):
-        text_relay_stage(u)
+    def image_stage(u):
         for h in range(CHUNKS):
             @pl.when(edge)
             def _():
@@ -195,159 +275,117 @@
                     image_copy(u + 1, h, img_nsem, near).start()
                     image_copy(u + 1, h, img_psem, partner).start()
 
-        if u < 2:
-            for h in range(SLICES):
-                text_copy(u, h).wait_recv()
-                if u == 0:
-                    text_start(1, h)
-                else:
-                    @pl.when(j >= 5)
-                    def _():
-                        text_start(2, h)
-        else:
-            @pl.when(j >= 5)
-            def _():
-                for h in range(SLICES):
-                    text_copy(2, h).wait_recv()
-
-    @pl.when(j < 5)
-    def _():
-        txt[3] = jnp.zeros((ROWS, WIDTH), BF16)
-
-    for s in range(4):
-        for h in range(CHUNKS):
-            image_arrival(1 - k, s, h)
-
-    p_sum[...] = jnp.zeros_like(p_sum)
-
-    @pl.loop(0, 4)
-    def _(s):
-        pair = img[:, s].reshape(2 * ROWS, WIDTH)
-        texts = txt[...].reshape(4 * ROWS, WIDTH)
-        logits = (
-            LOGIT_SCALE
-            * lax.dot_general(pair, texts, (((1,), (1,)), ((), ())), preferred_element_type=F32)
-            + BIAS_LOGIT
-        )
+    def text_stage(u):
+        for h in range(SLICES):
+            text_copy(u, h).wait_recv()
+            if u == 0:
+                text_start(1, h)
+            elif u == 1:
+                @pl.when(j >= 5)
+                def _():
+                    text_start(2, h)
+
+    def weights(logits, gap):
+        logits = LOGIT_SCALE * logits + BIAS_LOGIT
         row = lax.broadcasted_iota(jnp.int32, logits.shape, 0)
         col = lax.broadcasted_iota(jnp.int32, logits.shape, 1)
-        gap = 8 * (col // ROWS) + 4 * (row // ROWS) + (s - j)
+        gap = gap + 8 * (col // ROWS) + 4 * (row // ROWS)
         match = (gap == 0) & (lax.rem(row, ROWS) == lax.rem(col, ROWS))
         weight = jax.nn.sigmoid(jnp.where(match, -logits, logits))
         weight = jnp.where(match, -weight, weight)
-        weight = jnp.where((gap >= 0) & (gap <= 19), weight, 0.0)
-        wgt[...] = weight.astype(BF16)
+        return jnp.where((gap >= 0) & (gap <= 19), weight, 0.0).astype(BF16)
+
+    NT = (((1,), (1,)), ((), ()))
+    TN = (((0,), (0,)), ((), ()))
+
+    def products(t):
+        s = spot(t)
+        for h in range(CHUNKS):
+            image_arrival(1 - k, s, h)
+        pair = img[:, s].reshape(2 * ROWS, WIDTH)
+        texts = txt[0:3].reshape(3 * ROWS, WIDTH)
+        wgt[...] = weights(lax.dot_general(pair, texts, NT, preferred_element_type=F32), s - j)
         for n in range(WIDTH // COLS):
             part = pl.ds(n * COLS, COLS)
-            texts = txt[:, :, part].reshape(4 * ROWS, COLS)
+            texts = txt[0:3, :, part].reshape(3 * ROWS, COLS)
             q = jnp.dot(wgt[...], texts, preferred_element_type=F32)
             q_sum[:, s, :, part] = q.reshape(2, ROWS, COLS)
             pair = img[:, s, :, part].reshape(2 * ROWS, COLS)
-            p = lax.dot_general(wgt[...], pair, (((0,), (0,)), ((), ())), preferred_element_type=F32)
-            p_sum[:, :, part] += p.reshape(4, ROWS, COLS)
+            p = lax.dot_general(wgt[...], pair, TN, preferred_element_type=F32)
+            p_sum[0:3, :, part] += p.reshape(3, ROWS, COLS)
+
+        @pl.when(j >= 5)
+        def _():
+            old = weights(lax.dot_general(img[0, s], txt[3], NT, preferred_element_type=F32), 24 + s - j)
+            q_sum[0, s] += jnp.dot(old, txt[3], preferred_element_type=F32)
+            p_sum[3] += lax.dot_general(old, img[0, s], TN, preferred_element_type=F32)
+
         q_send[s] = q_sum[1 - k, s].astype(BF16)
         copy(q_send.at[s], q_recv.at[s], q_ssem.at[s], q_rsem.at[s], partner).start()
 
-    def back_copy(d, h):
-        return copy(p_send.at[d, thin(h)], p_recv.at[d, thin(h)], p_ssem.at[d, h], p_rsem.at[d, h], behind)
-
-    def back_start(d, h):
-        @pl.when(first)
-        def _():
-            copy(
-                p_send.at[d, thin(h)], back_hold.at[d], p_ssem.at[d, h], back_rsem.at[d], at(0, relay_place(h))
-            ).start()
-
-        @pl.when(jnp.logical_not(first))
-        def _():
-            back_copy(d, h).start()
-
-    def back_relay(d):
-        return copy(
-            back_hold.at[d], p_recv.at[d, thin(role)], back_ssem.at[d], p_rsem.at[d, role], prev_last
-        )
-
-    def back_relay_stage(d):
-        @pl.when(relay & (j >= 5) if d == 2 else relay)
-        def _():
-            copy(back_hold.at[d], back_hold.at[d], back_ssem.at[d], back_rsem.at[d], prev_last).wait_recv()
-            back_relay(d).start()
-
-    def far_copy(t, h, receiver):
-        s = spot(t)
-        sem = {"near": near_rsem, "far": far_rsem}[receiver]
-        dst = {"near": near_in, "far": far_in}[receiver]
-        return copy(far_out.at[s, rows(h)], dst.at[s, rows(h)], far_ssem.at[s, h], sem.at[s, h], far)
-
-    def near_copy(h):
-        s = spot(0)
-        return copy(near_out.at[rows(h)], far_in.at[s, rows(h)], near_ssem.at[h], far_rsem.at[s, h], near)
-
-    def near_arrival(t, h):
-        s = spot(t)
-        copy(far_out.at[s, rows(h)], near_in.at[s, rows(h)], far_ssem.at[s, h], near_rsem.at[s, h], far).wait_recv()
-
-    def far_arrival(t, h):
-        s = spot(t)
-        copy(far_out.at[s, rows(h)], far_in.at[s, rows(h)], far_ssem.at[s, h], far_rsem.at[s, h], far).wait_recv()
+    image_first(0)
+    text_relay_stage(0)
+    image_first(1)
+    p_sum[...] = jnp.zeros_like(p_sum)
+    for u in range(2):
+        if u > 0:
+            text_relay_stage(u)
+        image_stage(u)
+        text_stage(u)
+
+    @pl.when(middle)
+    def _():
+        for h in range(CHUNKS):
+            image_arrival(k, spot(3), h)
+            image_copy(3, h, img_nsem, near).start()
+            image_copy(3, h, img_psem, partner).start()
+
+    text_relay_stage(2)
 
     @pl.when(j >= 5)
     def _():
-        p_send[2] = p_sum[3].astype(BF16)
-        for h in range(SLICES):
-            back_start(2, h)
+        text_stage(2)
 
     @pl.loop(0, 4)
-    def _(s):
-        copy(q_send.at[s], q_recv.at[s], q_ssem.at[s], q_rsem.at[s], partner).wait_recv()
-
-    for u in range(3):
-        for h in range(CHUNKS):
-            r = rows(h)
-
-            @pl.when(edge)
-            def _():
-                t = spot(3 - u)
-                far_out[t, r] = (q_sum[k, t, r] + q_recv[t, r].astype(F32)).astype(BF16)
-                far_copy(3 - u, h, "near").start()
-
-            if u < 2:
-                @pl.when(middle)
-                def _():
-                    t = spot(3 - u)
-                    near_arrival(3 - u, h)
-                    total = q_sum[k, t, r] + q_recv[t, r].astype(F32) + near_in[t, r].astype(F32)
-                    far_out[t, r] = total.astype(BF16)
-                    far_copy(3 - u, h, "far").start()
-
-            if u == 1:
-                @pl.when(middle)
-                def _():
-                    t = spot(0)
-                    far_arrival(0, h)
-                    total = q_sum[k, t, r] + q_recv[t, r].astype(F32) + far_in[t, r].astype(F32)
-                    near_out[r] = total.astype(BF16)
-                    near_copy(h).start()
-
-        back_relay_stage(2 - u)
-        if u < 2:
-            for h in range(SLICES):
-                r = thin(h)
-                if u == 0:
-                    @pl.when(j >= 5)
-                    def _():
-                        back_copy(2, h).wait_recv()
-                        p_send[1, r] = (p_sum[2, r] + p_recv[2, r].astype(F32)).astype(BF16)
-                        back_start(1, h)
-
-                    @pl.when(j < 5)
-                    def _():
-                        p_send[1, r] = p_sum[2, r].astype(BF16)
-                        back_start(1, h)
-                else:
-                    back_copy(1, h).wait_recv()
-                    p_send[0, r] = (p_sum[1, r] + p_recv[1, r].astype(F32)).astype(BF16)
-                    back_start(0, h)
+    def _(i):
+        t = lax.rem(6 - i, 4)
+
+        @pl.when(edge & (i == 3))
+        def _():
+            for h in range(CHUNKS):
+                image_arrival(k, spot(3), h)
+                image_copy(3, h, img_psem, partner).start()
+            far_start(2)
+
+        products(t)
+
+    late = j >= 5
+    soon = j < 5
+
+    def when(condition, run, *args):
+        @pl.when(condition)
+        def _():
+            run(*args)
+
+    slow = last | (late & (place == 30))
+    when(late, back_begin, 3)
+    when(soon, back_begin, 2)
+    when(edge, far_start, 3)
+    when(late & jnp.logical_not(last), back_pass, 2)
+    when(middle, far_pass, 2)
+    when(relay & late, back_relay_stage, 2)
+    when(relay & soon, back_relay_stage, 1)
+    when(edge, far_start, 1)
+    when(jnp.logical_not(slow), back_pass, 1)
+    when(middle, far_pass, 3)
+    when(relay & late, back_relay_stage, 1)
+    when(relay & soon, back_relay_stage, 0)
+    when(middle, near_pass)
+    when(late & last, back_pass, 2)
+    when(slow, back_pass, 1)
+    when(relay & late, back_relay_stage, 0)
+    when(edge, sum_arrival, 0)
+    when(middle, sum_arrival, 1)
 
     for h in range(SLICES):
         back_copy(0, h).wait_recv()
@@ -421,7 +459,7 @@
             scratch_shapes=[
                 pltpu.VMEM((2, 4) + block, BF16),
                 pltpu.VMEM((4,) + block, BF16),
-                pltpu.VMEM((2 * ROWS, 4 * ROWS), BF16),
+                pltpu.VMEM((2 * ROWS, 3 * ROWS), BF16),
                 pltpu.VMEM((2, 4) + block, F32),
                 pltpu.VMEM((4,) + block, F32),
                 pltpu.VMEM((4,) + block, BF16),

time: 93.4 us -> 84.8 us (0.908)
  the two profiles are of different devices: /device:TPU:182 before, /device:TPU:127 now
where the time goes in v3:
time: 84.8 us; the launch traced here: 84.7 us
  Pallas kernels  81.6 us (96%)
  local copies, waits for them, and re-layouts  2.46 us (3%)
    pallas_call x1, Pallas kernels, per_device(): pl.pallas_call(lambda *refs: kernel(blocks, *refs), out_shape=(out, out),...  81.6 us
    unnamed x4, local copies, waits for them, and re-layouts  2.46 us

profile of v3, /device:TPU:127, one launch (start us, length us, event | category | flops | bytes accessed | tf_op | source)
XLA Modules:
  0.0 84.7 jit_solution(13885327191882822503)
XLA Ops:
  0.6 81.6 %pair_window.1 = (bf16[128,1152]{1,0:T(8,128)(2,1)}, bf16[128,1152]{1,0:T(8,128)(2,1)}) custom-call(bf16[128,1152]{1,0:T(8,128)(2,1)} %refs_0_.1, bf16[128,1152]{1,0:T(8,128)(2,1)} %refs_1_.1), custom_call_target="tpu_custom_call" | custom-call | tf_op jit(solution)/shard_map/pair_window/pallas_call | solution.py:454
  82.2 0.0 copy-start
  82.2 1.7 %copy.6 = bf16[128,1152]{1,0:T(8,128)(2,1)} copy(bf16[128,1152]{1,0:T(8,128)(2,1)} %get-tuple-element.4) | data formatting | bytes 589824
  83.9 0.0 copy-done
  84.0 0.7 copy.7
Async XLA Ops:
  82.2 1.8 %copy-start = (bf16[128,1152]{1,0:T(8,128)(2,1)S(1)}, bf16[128,1152]{1,0:T(8,128)(2,1)}, u32[]{:S(2)}) copy-start(bf16[128,1152]{1,0:T(8,128)(2,1)} %get-tuple-element.5) | copy-start | bytes 884740

commit v4 on v3

--- a/solution.py
+++ b/solution.py
@@ -13,9 +13,9 @@
 WIDTH = 1152
 CHUNKS = 2
 PIECE = ROWS // CHUNKS
-SLICES = 4
+SLICES = 8
 THIN = ROWS // SLICES
-RELAYS = ((24, 7, 1, 30), (23, 8, 15, 6))
+RELAYS = ((26, 14, 17, 30, 1, 16, 7, 24), (9, 5, 22, 8, 6, 25, 15, 23))
 COLS = 384
 F32 = jnp.float32
 BF16 = jnp.bfloat16
@@ -298,74 +298,102 @@
     NT = (((1,), (1,)), ((), ()))
     TN = (((0,), (0,)), ((), ()))
 
-    def products(t):
-        s = spot(t)
-        for h in range(CHUNKS):
-            image_arrival(1 - k, s, h)
+    def products(t, first_text, texts):
+        s = spot(t)
+        part_w = wgt.at[:, pl.ds(0, texts * ROWS)]
+        near_texts = pl.ds(first_text, texts)
         pair = img[:, s].reshape(2 * ROWS, WIDTH)
-        texts = txt[0:3].reshape(3 * ROWS, WIDTH)
-        wgt[...] = weights(lax.dot_general(pair, texts, NT, preferred_element_type=F32), s - j)
+        block = txt[near_texts].reshape(texts * ROWS, WIDTH)
+        logits = lax.dot_general(pair, block, NT, preferred_element_type=F32)
+        part_w[...] = weights(logits, 8 * first_text + s - j)
         for n in range(WIDTH // COLS):
             part = pl.ds(n * COLS, COLS)
-            texts = txt[0:3, :, part].reshape(3 * ROWS, COLS)
-            q = jnp.dot(wgt[...], texts, preferred_element_type=F32)
-            q_sum[:, s, :, part] = q.reshape(2, ROWS, COLS)
+            block = txt[near_texts, :, part].reshape(texts * ROWS, COLS)
+            q = jnp.dot(part_w[...], block, preferred_element_type=F32).reshape(2, ROWS, COLS)
             pair = img[:, s, :, part].reshape(2 * ROWS, COLS)
-            p = lax.dot_general(wgt[...], pair, TN, preferred_element_type=F32)
-            p_sum[0:3, :, part] += p.reshape(3, ROWS, COLS)
-
-        @pl.when(j >= 5)
-        def _():
+            p = lax.dot_general(part_w[...], pair, TN, preferred_element_type=F32)
+            if first_text == 0:
+                q_sum[:, s, :, part] = q
+            else:
+                q_sum[:, s, :, part] += q
+            p_sum[near_texts, :, part] += p.reshape(texts, ROWS, COLS)
+
+    def recent(t):
+        s = spot(t)
+        for h in range(CHUNKS):
+            image_arrival(1 - k, s, h)
+        products(t, 0, 2)
+
+    def share(s):
+        q_send[s] = q_sum[1 - k, s].astype(BF16)
+        copy(q_send.at[s], q_recv.at[s], q_ssem.at[s], q_rsem.at[s], partner).start()
+
+    def older(t):
+        products(t, 2, 1)
+
+        @pl.when((j < 5) | (spot(t) >= z))
+        def _():
+            share(spot(t))
+
+    def oldest(start, stop):
+        @pl.loop(start, stop)
+        def _(s):
             old = weights(lax.dot_general(img[0, s], txt[3], NT, preferred_element_type=F32), 24 + s - j)
             q_sum[0, s] += jnp.dot(old, txt[3], preferred_element_type=F32)
             p_sum[3] += lax.dot_general(old, img[0, s], TN, preferred_element_type=F32)
-
-        q_send[s] = q_sum[1 - k, s].astype(BF16)
-        copy(q_send.at[s], q_recv.at[s], q_ssem.at[s], q_rsem.at[s], partner).start()
+            share(s)
+
+    late = j >= 5
+    soon = j < 5
+
+    def when(condition, run, *args):
+        @pl.when(condition)
+        def _():
+            run(*args)
 
     image_first(0)
     text_relay_stage(0)
     image_first(1)
     p_sum[...] = jnp.zeros_like(p_sum)
-    for u in range(2):
-        if u > 0:
-            text_relay_stage(u)
-        image_stage(u)
-        text_stage(u)
-
-    @pl.when(middle)
-    def _():
-        for h in range(CHUNKS):
-            image_arrival(k, spot(3), h)
-            image_copy(3, h, img_nsem, near).start()
-            image_copy(3, h, img_psem, partner).start()
-
+    image_stage(0)
+    when(middle, image_stage, 1)
+    when(middle & first, image_stage, 2)
+    text_stage(0)
+
+    @pl.loop(0, 2 + z * (3 - z) // 2)
+    def _(i):
+        recent(jnp.where(i < 2, 1 - i, 2))
+
+    text_relay_stage(1)
+    when(edge, image_stage, 1)
+    when(middle & jnp.logical_not(first), image_stage, 2)
+    text_stage(1)
     text_relay_stage(2)
-
-    @pl.when(j >= 5)
+    when(edge, recent, 2)
+
+    @pl.loop(0, 3)
+    def _(i):
+        older(2 - i)
+
+    when(edge, image_stage, 2)
+
+    @pl.when(late & edge)
     def _():
         text_stage(2)
-
-    @pl.loop(0, 4)
-    def _(i):
-        t = lax.rem(6 - i, 4)
-
-        @pl.when(edge & (i == 3))
-        def _():
-            for h in range(CHUNKS):
-                image_arrival(k, spot(3), h)
-                image_copy(3, h, img_psem, partner).start()
-            far_start(2)
-
-        products(t)
-
-    late = j >= 5
-    soon = j < 5
-
-    def when(condition, run, *args):
-        @pl.when(condition)
-        def _():
-            run(*args)
+        oldest(1, 3)
+
+    when(edge, far_start, 2)
+    recent(3)
+    older(3)
+
+    @pl.when(late & middle)
+    def _():
+        text_stage(2)
+
+    @pl.when(late)
+    def _():
+        oldest(0, jnp.where(middle, z, 1))
+
 
     slow = last | (late & (place == 30))
     when(late, back_begin, 3)
@@ -375,11 +403,13 @@
     when(middle, far_pass, 2)
     when(relay & late, back_relay_stage, 2)
     when(relay & soon, back_relay_stage, 1)
-    when(edge, far_start, 1)
+    hold = relay & (z == 3)
+    when(edge & jnp.logical_not(hold), far_start, 1)
     when(jnp.logical_not(slow), back_pass, 1)
     when(middle, far_pass, 3)
     when(relay & late, back_relay_stage, 1)
     when(relay & soon, back_relay_stage, 0)
+    when(hold, far_start, 1)
     when(middle, near_pass)
     when(late & last, back_pass, 2)
     when(slow, back_pass, 1)

time: 84.8 us -> 78.5 us (0.926)
  the two profiles are of different devices: /device:TPU:127 before, /device:TPU:1 now
where the time goes in v4:
time: 78.5 us; the launch traced here: 78.3 us
  Pallas kernels  75.2 us (96%)
  local copies, waits for them, and re-layouts  2.46 us (3%)
    pallas_call x1, Pallas kernels, per_device(): pl.pallas_call(lambda *refs: kernel(blocks, *refs), out_shape=(out, out),...  75.2 us
    unnamed x4, local copies, waits for them, and re-layouts  2.46 us

profile of v4, /device:TPU:1, one launch (start us, length us, event | category | flops | bytes accessed | tf_op | source)
XLA Modules:
  0.0 78.3 jit_solution(7253827092673815805)
XLA Ops:
  0.6 75.2 %pair_window.1 = (bf16[128,1152]{1,0:T(8,128)(2,1)}, bf16[128,1152]{1,0:T(8,128)(2,1)}) custom-call(bf16[128,1152]{1,0:T(8,128)(2,1)} %refs_0_.1, bf16[128,1152]{1,0:T(8,128)(2,1)} %refs_1_.1), custom_call_target="tpu_custom_call" | custom-call | tf_op jit(solution)/shard_map/pair_window/pallas_call | solution.py:484
  75.9 0.0 copy-start
  75.9 1.7 %copy.6 = bf16[128,1152]{1,0:T(8,128)(2,1)} copy(bf16[128,1152]{1,0:T(8,128)(2,1)} %get-tuple-element.4) | data formatting | bytes 589824
  77.6 0.0 copy-done
  77.6 0.7 copy.7
Async XLA Ops:
  75.9 1.8 %copy-start = (bf16[128,1152]{1,0:T(8,128)(2,1)S(1)}, bf16[128,1152]{1,0:T(8,128)(2,1)}, u32[]{:S(2)}) copy-start(bf16[128,1152]{1,0:T(8,128)(2,1)} %get-tuple-element.5) | copy-start | bytes 884740

commit v5 on v4

--- a/solution.py
+++ b/solution.py
@@ -11,11 +11,11 @@
 EPSILON = 1e-06
 ROWS = 128
 WIDTH = 1152
-CHUNKS = 2
+CHUNKS = 4
 PIECE = ROWS // CHUNKS
 SLICES = 8
 THIN = ROWS // SLICES
-RELAYS = ((26, 14, 17, 30, 1, 16, 7, 24), (9, 5, 22, 8, 6, 25, 15, 23))
+RELAYS = ((26, 14, 17, 29, 1, 16, 7, 24), (9, 5, 22, 8, 6, 25, 15, 23))
 COLS = 384
 F32 = jnp.float32
 BF16 = jnp.bfloat16
@@ -37,13 +37,14 @@
 
 def kernel(
     blocks,
-    image_ref, text_ref, image_out, text_out,
+    image_in, text_in, image_out, text_out,
+    image_ref, text_ref, in_sem,
     img, txt, wgt, q_sum, p_sum,
     q_send, q_recv, far_out, near_out, near_in, far_in, p_send, p_recv,
     fwd_hold, back_hold,
     txt_ssem, txt_rsem, img_fsem, img_nsem, img_psem, img_rsem,
     q_ssem, q_rsem, far_ssem, near_ssem, near_rsem, far_rsem, p_ssem, p_rsem,
-    fwd_ssem, fwd_rsem, back_ssem, back_rsem,
+    ante_ssem, fwd_ssem, fwd_rsem, back_ssem, back_rsem, fwd_ready, back_ready, lane_ready,
 ):
     blk = lax.axis_index("blk")
     z = lax.axis_index("grp")
@@ -62,6 +63,7 @@
     place = lax.rem(column, 32)
     first = place == 0
     last = place == 31
+    ante = place == 30
 
     def relay_place(h):
         return RELAYS[0][h] + k * (RELAYS[1][h] - RELAYS[0][h])
@@ -75,7 +77,7 @@
         role = role + jnp.where(match, h, 0)
         relay = relay | match
     next_first, own_first = at(1, 0), at(0, 0)
-    prev_last, own_last = at(blocks // 64 - 1, 31), at(0, 31)
+    prev_last, own_last, own_ante = at(blocks // 64 - 1, 31), at(0, 31), at(0, 30)
 
     partner = (blk + 1 - 2 * k, z)
     ahead = (lax.rem(blk + 2, blocks), z)
@@ -83,6 +85,11 @@
     far = (blk, z + sign)
     near = (blk, z - sign)
 
+    def when(condition, run, *args):
+        @pl.when(condition)
+        def _():
+            run(*args)
+
     def copy(src, dst, ssem, rsem, device):
         return pltpu.make_async_remote_copy(
             src_ref=src, dst_ref=dst, send_sem=ssem, recv_sem=rsem, device_id=device, device_id_type=MESH
@@ -94,6 +101,11 @@
     def thin(h):
         return pl.ds(pl.multiple_of(h * THIN, THIN), THIN)
 
+    image_load = pltpu.make_async_copy(image_in, image_ref, in_sem.at[0])
+    text_load = pltpu.make_async_copy(text_in, text_ref, in_sem.at[1])
+    image_load.start()
+    text_load.start()
+
     barrier = pltpu.get_barrier_semaphore()
 
     def greet(condition, devices):
@@ -102,22 +114,48 @@
             for device in devices:
                 pl.semaphore_signal(barrier, inc=1, device_id=device, device_id_type=MESH)
 
-    greet(relay, (own_last, own_first))
-    greet(first, [at(blocks // 64 - 1, relay_place(h)) for h in range(SLICES)])
-    greet(last, [at(1, relay_place(h)) for h in range(SLICES)])
+    thirds = blocks // 64
+    early, final = third == 0, third == thirds - 1
+    not_early, not_final = jnp.logical_not(early), jnp.logical_not(final)
+    past_relays = [at(thirds - 1, relay_place(h)) for h in range(SLICES)]
+    coming_relays = [at(1, relay_place(h)) for h in range(SLICES)]
+    own_relays = [at(0, relay_place(h)) for h in range(SLICES)]
+    greet(relay, (own_last, own_ante))
+    greet(first, own_relays)
+    greet(first & early, past_relays)
+    greet(last & not_final, coming_relays)
+    greet(relay & not_final, (next_first,))
+    greet(relay & early, (prev_last,))
     for device in (partner, far):
         pl.semaphore_signal(barrier, inc=1, device_id=device, device_id_type=MESH)
     greet(middle, (near,))
     greet(jnp.logical_not(first), (behind,))
     greet(jnp.logical_not(last), (ahead,))
 
+    image_load.wait()
     unit, _ = unit_and_inverse(image_ref)
     img[k, z] = unit.astype(BF16)
+    text_load.wait()
     unit, _ = unit_and_inverse(text_ref)
     txt[0] = unit.astype(BF16)
 
-    greeted = 4 + z * (3 - z) // 2 + jnp.where(relay, 2, 0) + jnp.where(first | last, SLICES - 1, 0)
+    answer_first, answer_last = first & not_early, last & final
+    greeted = 4 + z * (3 - z) // 2 + jnp.where(last, SLICES - 1, 0) - jnp.where(first, 1, 0)
+    greeted = greeted + jnp.where(answer_first | answer_last | ante, SLICES, 0)
+    greeted = greeted + jnp.where(relay & final, 1, 0) + jnp.where(relay & not_early, 1, 0) + jnp.where(relay, 1, 0)
     pl.semaphore_wait(barrier, greeted)
+
+    when(relay, lambda: pl.semaphore_signal(lane_ready, inc=1, device_id=own_first, device_id_type=MESH))
+
+    @pl.when(answer_first)
+    def _():
+        for device in past_relays:
+            pl.semaphore_signal(fwd_ready, inc=1, device_id=device, device_id_type=MESH)
+
+    @pl.when(answer_last)
+    def _():
+        for device in coming_relays:
+            pl.semaphore_signal(back_ready, inc=1, device_id=device, device_id_type=MESH)
 
     def image_copy(t, h, ssem, device):
         s = spot(t)
@@ -133,16 +171,26 @@
             txt.at[d, thin(h)], txt.at[d + 1, thin(h)], txt_ssem.at[d, h], txt_rsem.at[d, h], ahead
         )
 
+    def relay_copy(d, hold, h, ssem):
+        return copy(txt.at[d, thin(h)], fwd_hold.at[hold], ssem, fwd_rsem.at[hold], at(0, relay_place(h)))
+
+    def ante_copy(d, h):
+        return relay_copy(d, d + 1, h, ante_ssem.at[d, h])
+
     def text_start(d, h):
-        @pl.when(last)
-        def _():
-            copy(
-                txt.at[d, thin(h)], fwd_hold.at[d], txt_ssem.at[d, h], fwd_rsem.at[d], at(0, relay_place(h))
-            ).start()
+        if d == 1:
+            @pl.when(ante & (j >= 5))
+            def _():
+                ante_copy(1, h).start()
 
         @pl.when(jnp.logical_not(last))
         def _():
             text_copy(d, h).start()
+
+        if d == 0:
+            @pl.when(last)
+            def _():
+                relay_copy(0, 0, h, txt_ssem.at[0, h]).start()
 
     def text_relay(d):
         return copy(
@@ -150,10 +198,11 @@
         )
 
     def text_relay_stage(d):
-        @pl.when(relay & (j >= 5) if d == 2 else relay)
-        def _():
-            copy(fwd_hold.at[d], fwd_hold.at[d], fwd_ssem.at[d], fwd_rsem.at[d], next_first).wait_recv()
-            text_relay(d).start()
+        copy(fwd_hold.at[d], fwd_hold.at[d], fwd_ssem.at[d], fwd_rsem.at[d], next_first).wait_recv()
+        text_relay(d).start()
+
+    for h in range(SLICES):
+        when(ante, lambda h=h: ante_copy(0, h).start())
 
     for h in range(SLICES):
         text_start(0, h)
@@ -346,29 +395,31 @@
     late = j >= 5
     soon = j < 5
 
-    def when(condition, run, *args):
-        @pl.when(condition)
-        def _():
-            run(*args)
-
-    image_first(0)
-    text_relay_stage(0)
-    image_first(1)
+    for h in range(CHUNKS // 2):
+        image_first(h)
+    when(relay & not_final & not_early, pl.semaphore_wait, fwd_ready, 1)
+    when(relay & not_early, text_relay_stage, 0)
+    when(relay & not_early, text_relay_stage, 1)
+    for h in range(CHUNKS // 2, CHUNKS):
+        image_first(h)
     p_sum[...] = jnp.zeros_like(p_sum)
     image_stage(0)
+    when(relay & early, pl.semaphore_wait, fwd_ready, 1)
+    when(relay & early, text_relay_stage, 0)
+    when(relay & early, text_relay_stage, 1)
     when(middle, image_stage, 1)
     when(middle & first, image_stage, 2)
     text_stage(0)
 
+    when(relay & late, text_relay_stage, 2)
+
     @pl.loop(0, 2 + z * (3 - z) // 2)
     def _(i):
         recent(jnp.where(i < 2, 1 - i, 2))
 
-    text_relay_stage(1)
     when(edge, image_stage, 1)
     when(middle & jnp.logical_not(first), image_stage, 2)
     text_stage(1)
-    text_relay_stage(2)
     when(edge, recent, 2)
 
     @pl.loop(0, 3)
@@ -395,25 +446,32 @@
         oldest(0, jnp.where(middle, z, 1))
 
 
+    when(first, pl.semaphore_wait, lane_ready, SLICES)
     slow = last | (late & (place == 30))
+    def relay_step(n, here):
+        when(relay & late & here, back_relay_stage, 2 - n)
+        if n < 2:
+            when(relay & soon & here, back_relay_stage, 1 - n)
+
     when(late, back_begin, 3)
     when(soon, back_begin, 2)
+    relay_step(0, not_early)
     when(edge, far_start, 3)
     when(late & jnp.logical_not(last), back_pass, 2)
     when(middle, far_pass, 2)
-    when(relay & late, back_relay_stage, 2)
-    when(relay & soon, back_relay_stage, 1)
+    when(relay & early, pl.semaphore_wait, back_ready, 1)
+    relay_step(0, early)
     hold = relay & (z == 3)
     when(edge & jnp.logical_not(hold), far_start, 1)
     when(jnp.logical_not(slow), back_pass, 1)
+    relay_step(1, not_early)
     when(middle, far_pass, 3)
-    when(relay & late, back_relay_stage, 1)
-    when(relay & soon, back_relay_stage, 0)
+    relay_step(1, early)
     when(hold, far_start, 1)
+    relay_step(2, True)
     when(middle, near_pass)
     when(late & last, back_pass, 2)
     when(slow, back_pass, 1)
-    when(relay & late, back_relay_stage, 0)
     when(edge, sum_arrival, 0)
     when(middle, sum_arrival, 1)
 
@@ -445,8 +503,18 @@
         @pl.when(j >= (5 if d == 2 else 0))
         def _():
             for h in range(SLICES):
+                back_copy(d, h).wait_send()
+
+        @pl.when((j >= (5 if d == 2 else 0)) & ((d == 0) | jnp.logical_not(last)))
+        def _():
+            for h in range(SLICES):
                 text_copy(d, h).wait_send()
-                back_copy(d, h).wait_send()
+
+        if d < 2:
+            @pl.when(ante & (j >= 5) if d == 1 else ante)
+            def _():
+                for h in range(SLICES):
+                    ante_copy(d, h).wait_send()
 
     for h in range(CHUNKS):
         for t in range(4):
@@ -484,9 +552,12 @@
         return pl.pallas_call(
             lambda *refs: kernel(blocks, *refs),
             out_shape=(out, out),
-            in_specs=[vmem, vmem],
+            in_specs=[pl.BlockSpec(memory_space=pl.ANY)] * 2,
             out_specs=(vmem, vmem),
             scratch_shapes=[
+                pltpu.VMEM(block, BF16),
+                pltpu.VMEM(block, BF16),
+                dma((2,)),
                 pltpu.VMEM((2, 4) + block, BF16),
                 pltpu.VMEM((4,) + block, BF16),
                 pltpu.VMEM((2 * ROWS, 3 * ROWS), BF16),
@@ -516,10 +587,14 @@
                 dma((4, CHUNKS)),
                 dma((3, SLICES)),
                 dma((3, SLICES)),
+                dma((2, SLICES)),
                 dma((3,)),
                 dma((3,)),
                 dma((3,)),
                 dma((3,)),
+                pltpu.SemaphoreType.REGULAR,
+                pltpu.SemaphoreType.REGULAR,
+                pltpu.SemaphoreType.REGULAR,
             ],
             compiler_params=pltpu.CompilerParams(
                 collective_id=0, has_side_effects=True, vmem_limit_bytes=56 * 1024 * 1024

time: 78.5 us -> 75.4 us (0.961)
  Pallas kernels: 75.2 us -> 71.6 us
    pallas_call x1, Pallas kernels: 75.2 us -> 71.6 us  [per_device(): pl.pallas_call(lambda *refs: kernel(blocks, *refs), out_shape=(out, out),...]
where the time goes in v5:
time: 75.4 us; the launch traced here: 74.7 us
  Pallas kernels  71.6 us (95%)
  local copies, waits for them, and re-layouts  2.46 us (3%)
    pallas_call x1, Pallas kernels, per_device(): pl.pallas_call(lambda *refs: kernel(blocks, *refs), out_shape=(out, out),...  71.6 us
    unnamed x4, local copies, waits for them, and re-layouts  2.46 us

profile of v5, /device:TPU:1, one launch (start us, length us, event | category | flops | bytes accessed | tf_op | source)
XLA Modules:
  0.0 74.7 jit_solution(16233596375114964405)
XLA Ops:
  0.6 71.6 %pair_window.1 = (bf16[128,1152]{1,0:T(8,128)(2,1)}, bf16[128,1152]{1,0:T(8,128)(2,1)}) custom-call(bf16[128,1152]{1,0:T(8,128)(2,1)} %refs_0_.1, bf16[128,1152]{1,0:T(8,128)(2,1)} %refs_1_.1), custom_call_target="tpu_custom_call" | custom-call | tf_op jit(solution)/shard_map/pair_window/pallas_call | solution.py:552
  72.2 0.0 copy-start
  72.2 1.7 %copy.6 = bf16[128,1152]{1,0:T(8,128)(2,1)} copy(bf16[128,1152]{1,0:T(8,128)(2,1)} %get-tuple-element.4) | data formatting | bytes 589824
  74.0 0.0 copy-done
  74.0 0.7 copy.7
Async XLA Ops:
  72.2 1.8 %copy-start = (bf16[128,1152]{1,0:T(8,128)(2,1)S(1)}, bf16[128,1152]{1,0:T(8,128)(2,1)}, u32[]{:S(2)}) copy-start(bf16[128,1152]{1,0:T(8,128)(2,1)} %get-tuple-element.5) | copy-start | bytes 884740

commit v6 on v5

--- a/solution.py
+++ b/solution.py
@@ -15,7 +15,7 @@
 PIECE = ROWS // CHUNKS
 SLICES = 8
 THIN = ROWS // SLICES
-RELAYS = ((26, 14, 17, 29, 1, 16, 7, 24), (9, 5, 22, 8, 6, 25, 15, 23))
+RELAYS = ((26, 14, 17, 29, 2, 16, 7, 24), (9, 5, 22, 8, 6, 25, 15, 23))
 COLS = 384
 F32 = jnp.float32
 BF16 = jnp.bfloat16
@@ -28,8 +28,10 @@
     return wide * inverse, inverse
 
 
-def undo(total, ref):
-    unit, inverse = unit_and_inverse(ref)
+def undo(total, wide):
+    wide = wide.astype(F32)
+    inverse = 1.0 / jnp.sqrt(jnp.sum(wide * wide, axis=-1, keepdims=True) + EPSILON)
+    unit = wide * inverse
     grad = LOGIT_SCALE * total
     inner = jnp.sum(unit * grad, axis=-1, keepdims=True)
     return ((grad - unit * inner) * inverse).astype(BF16)
@@ -38,11 +40,11 @@
 def kernel(
     blocks,
     image_in, text_in, image_out, text_out,
-    image_ref, text_ref, in_sem,
+    image_ref, text_ref, in_sem, out_held, out_sem,
     img, txt, wgt, q_sum, p_sum,
     q_send, q_recv, far_out, near_out, near_in, far_in, p_send, p_recv,
     fwd_hold, back_hold,
-    txt_ssem, txt_rsem, img_fsem, img_nsem, img_psem, img_rsem,
+    txt_ssem, txt_rsem, img_fsem, img_nsem, img_psem, img_rsem, pair_rsem,
     q_ssem, q_rsem, far_ssem, near_ssem, near_rsem, far_rsem, p_ssem, p_rsem,
     ante_ssem, fwd_ssem, fwd_rsem, back_ssem, back_rsem, fwd_ready, back_ready, lane_ready,
 ):
@@ -160,29 +162,29 @@
     def image_copy(t, h, ssem, device):
         s = spot(t)
         ref = img.at[k, s, rows(h)]
-        return copy(ref, ref, ssem.at[t, h], img_rsem.at[k, s, h], device)
-
-    def image_arrival(kk, s, h):
-        ref = img.at[kk, s, rows(h)]
-        copy(ref, ref, img_psem.at[0, h], img_rsem.at[kk, s, h], partner).wait_recv()
+        return copy(ref, ref, ssem.at[t], img_rsem.at[s, h], device)
+
+    def to_partner(t, h):
+        s = spot(t)
+        ref = img.at[k, s, rows(h)]
+        copy(ref, ref, img_psem.at[t], pair_rsem.at[s], partner).start()
+
+    def image_arrival(s, h):
+        ref = img.at[k, s, rows(h)]
+        copy(ref, ref, img_psem.at[0], img_rsem.at[s, h], partner).wait_recv()
 
     def text_copy(d, h):
         return copy(
-            txt.at[d, thin(h)], txt.at[d + 1, thin(h)], txt_ssem.at[d, h], txt_rsem.at[d, h], ahead
+            txt.at[d, thin(h)], txt.at[d + 1, thin(h)], txt_ssem.at[d], txt_rsem.at[d, h], ahead
         )
 
     def relay_copy(d, hold, h, ssem):
         return copy(txt.at[d, thin(h)], fwd_hold.at[hold], ssem, fwd_rsem.at[hold], at(0, relay_place(h)))
 
     def ante_copy(d, h):
-        return relay_copy(d, d + 1, h, ante_ssem.at[d, h])
+        return relay_copy(d, d + 1, h, ante_ssem.at[d])
 
     def text_start(d, h):
-        if d == 1:
-            @pl.when(ante & (j >= 5))
-            def _():
-                ante_copy(1, h).start()
-
         @pl.when(jnp.logical_not(last))
         def _():
             text_copy(d, h).start()
@@ -190,7 +192,7 @@
         if d == 0:
             @pl.when(last)
             def _():
-                relay_copy(0, 0, h, txt_ssem.at[0, h]).start()
+                relay_copy(0, 0, h, txt_ssem.at[0]).start()
 
     def text_relay(d):
         return copy(
@@ -208,13 +210,13 @@
         text_start(0, h)
 
     def back_copy(d, h):
-        return copy(p_send.at[d, thin(h)], p_recv.at[d, thin(h)], p_ssem.at[d, h], p_rsem.at[d, h], behind)
+        return copy(p_send.at[d, thin(h)], p_recv.at[d, thin(h)], p_ssem.at[d], p_rsem.at[d, h], behind)
 
     def back_start(d, h):
         @pl.when(first)
         def _():
             copy(
-                p_send.at[d, thin(h)], back_hold.at[d], p_ssem.at[d, h], back_rsem.at[d], at(0, relay_place(h))
+                p_send.at[d, thin(h)], back_hold.at[d], p_ssem.at[d], back_rsem.at[d], at(0, relay_place(h))
             ).start()
 
         @pl.when(jnp.logical_not(first))
@@ -234,19 +236,19 @@
         s = spot(t)
         sem = {"near": near_rsem, "far": far_rsem}[receiver]
         dst = {"near": near_in, "far": far_in}[receiver]
-        return copy(far_out.at[s, rows(h)], dst.at[s, rows(h)], far_ssem.at[s, h], sem.at[s, h], far)
+        return copy(far_out.at[s, rows(h)], dst.at[s, rows(h)], far_ssem.at[s], sem.at[s, h], far)
 
     def near_copy(h):
         s = spot(0)
-        return copy(near_out.at[rows(h)], far_in.at[s, rows(h)], near_ssem.at[h], far_rsem.at[s, h], near)
+        return copy(near_out.at[rows(h)], far_in.at[s, rows(h)], near_ssem, far_rsem.at[s, h], near)
 
     def near_arrival(t, h):
         s = spot(t)
-        copy(far_out.at[s, rows(h)], near_in.at[s, rows(h)], far_ssem.at[s, h], near_rsem.at[s, h], far).wait_recv()
+        copy(far_out.at[s, rows(h)], near_in.at[s, rows(h)], far_ssem.at[s], near_rsem.at[s, h], far).wait_recv()
 
     def far_arrival(t, h):
         s = spot(t)
-        copy(far_out.at[s, rows(h)], far_in.at[s, rows(h)], far_ssem.at[s, h], far_rsem.at[s, h], far).wait_recv()
+        copy(far_out.at[s, rows(h)], far_in.at[s, rows(h)], far_ssem.at[s], far_rsem.at[s, h], far).wait_recv()
 
     def sum_arrival(t):
         s = spot(t)
@@ -298,41 +300,48 @@
         @pl.when(edge)
         def _():
             image_copy(0, h, img_fsem, far).start()
-            image_copy(0, h, img_psem, partner).start()
+            to_partner(0, h)
 
         @pl.when(middle)
         def _():
             image_copy(1, h, img_fsem, far).start()
             image_copy(1, h, img_nsem, near).start()
-            image_copy(1, h, img_psem, partner).start()
+            to_partner(1, h)
 
     def image_stage(u):
         for h in range(CHUNKS):
             @pl.when(edge)
             def _():
-                image_arrival(k, spot(u + 1), h)
-                image_copy(u + 1, h, img_psem, partner).start()
+                image_arrival(spot(u + 1), h)
+                to_partner(u + 1, h)
 
             @pl.when(middle)
             def _():
                 if u == 0:
-                    image_arrival(k, spot(0), h)
+                    image_arrival(spot(0), h)
                     image_copy(0, h, img_fsem, far).start()
-                    image_copy(0, h, img_psem, partner).start()
+                    to_partner(0, h)
                 else:
-                    image_arrival(k, spot(u + 1), h)
+                    image_arrival(spot(u + 1), h)
                     image_copy(u + 1, h, img_nsem, near).start()
-                    image_copy(u + 1, h, img_psem, partner).start()
+                    to_partner(u + 1, h)
 
     def text_stage(u):
         for h in range(SLICES):
             text_copy(u, h).wait_recv()
             if u == 0:
-                text_start(1, h)
+                when(ante & (j >= 5), lambda h=h: ante_copy(1, h).start())
+                when(jnp.logical_not(ante & (j >= 5)), text_start, 1, h)
             elif u == 1:
                 @pl.when(j >= 5)
                 def _():
                     text_start(2, h)
+
+        if u == 0:
+            @pl.when(ante & (j >= 5))
+            def _():
+                for h in range(SLICES):
+                    text_start(1, h)
 
     def weights(logits, gap):
         logits = LOGIT_SCALE * logits + BIAS_LOGIT
@@ -369,8 +378,8 @@
 
     def recent(t):
         s = spot(t)
-        for h in range(CHUNKS):
-            image_arrival(1 - k, s, h)
+        ref = img.at[1 - k, s]
+        copy(ref, ref, img_psem.at[t], pair_rsem.at[s], partner).wait_recv()
         products(t, 0, 2)
 
     def share(s):
@@ -475,70 +484,71 @@
     when(edge, sum_arrival, 0)
     when(middle, sum_arrival, 1)
 
-    for h in range(SLICES):
-        back_copy(0, h).wait_recv()
-    text_out[...] = undo(p_sum[0] + p_recv[0].astype(F32), text_ref)
+    def finish(which, h, total):
+        r = rows(h)
+        out_held[which, r] = undo(total, (image_ref, text_ref)[which][r])
+        out_copy(which, h).start()
+
+    def out_copy(which, h):
+        r = rows(h)
+        return pltpu.make_async_copy(out_held.at[which, r], (image_out, text_out)[which].at[r], out_sem.at[which])
+
+    for h in range(CHUNKS):
+        for i in range(SLICES // CHUNKS):
+            back_copy(0, SLICES // CHUNKS * h + i).wait_recv()
+        finish(1, h, p_sum[0, rows(h)] + p_recv[0, rows(h)].astype(F32))
+
+    for h in range(CHUNKS):
+        r = rows(h)
+
+        @pl.when(edge)
+        def _():
+            far_arrival(0, h)
+            finish(0, h, own_part(z, r) + far_in[z, r].astype(F32))
+
+        @pl.when(middle)
+        def _():
+            near_arrival(1, h)
+            far_arrival(1, h)
+            finish(0, h, own_part(z, r) + near_in[z, r].astype(F32) + far_in[z, r].astype(F32))
+
+    def sent(block, ssem):
+        copy(block, block, ssem, img_rsem.at[0, 0], partner).wait_send()
+
+    for which in range(2):
+        pltpu.make_async_copy(out_held.at[which], (image_out, text_out)[which], out_sem.at[which]).wait()
+
+    for d in range(3):
+        used = late if d == 2 else True
+        when(relay & used, lambda: text_relay(d).wait_send())
+        when(relay & used, lambda: back_relay(d).wait_send())
+        when((j >= 0) & used, sent, p_send.at[d], p_ssem.at[d])
+        when((j >= 0) & used if d == 0 else jnp.logical_not(last) & used, sent, txt.at[d], txt_ssem.at[d])
+        if d < 2:
+            when(ante & (late if d == 1 else True), sent, txt.at[d], ante_ssem.at[d])
+
+    for t in range(4):
+        sent(img.at[k, spot(t)], img_psem.at[t])
 
     @pl.when(edge)
     def _():
-        for h in range(CHUNKS):
-            far_arrival(0, h)
-        total = q_sum[k, z] + q_recv[z].astype(F32) + far_in[z].astype(F32)
-        image_out[...] = undo(total, image_ref)
+        sent(img.at[k, spot(0)], img_fsem.at[0])
+        for t in (1, 2, 3):
+            sent(far_out.at[spot(t)], far_ssem.at[spot(t)])
 
     @pl.when(middle)
     def _():
-        for h in range(CHUNKS):
-            near_arrival(1, h)
-            far_arrival(1, h)
-        total = q_sum[k, z] + q_recv[z].astype(F32) + near_in[z].astype(F32) + far_in[z].astype(F32)
-        image_out[...] = undo(total, image_ref)
-
-    for d in range(3):
-        @pl.when(relay & (j >= 5) if d == 2 else relay)
-        def _():
-            text_relay(d).wait_send()
-            back_relay(d).wait_send()
-
-        @pl.when(j >= (5 if d == 2 else 0))
-        def _():
-            for h in range(SLICES):
-                back_copy(d, h).wait_send()
-
-        @pl.when((j >= (5 if d == 2 else 0)) & ((d == 0) | jnp.logical_not(last)))
-        def _():
-            for h in range(SLICES):
-                text_copy(d, h).wait_send()
-
-        if d < 2:
-            @pl.when(ante & (j >= 5) if d == 1 else ante)
-            def _():
-                for h in range(SLICES):
-                    ante_copy(d, h).wait_send()
-
-    for h in range(CHUNKS):
-        for t in range(4):
-            image_copy(t, h, img_psem, partner).wait_send()
-
-        @pl.when(edge)
-        def _():
-            image_copy(0, h, img_fsem, far).wait_send()
-            for t in (1, 2, 3):
-                far_copy(t, h, "near").wait_send()
-
-        @pl.when(middle)
-        def _():
-            for t in (0, 1):
-                image_copy(t, h, img_fsem, far).wait_send()
-            for t in (1, 2, 3):
-                image_copy(t, h, img_nsem, near).wait_send()
-            for t in (2, 3):
-                far_copy(t, h, "far").wait_send()
-            near_copy(h).wait_send()
+        for t in (0, 1):
+            sent(img.at[k, spot(t)], img_fsem.at[t])
+        for t in (1, 2, 3):
+            sent(img.at[k, spot(t)], img_nsem.at[t])
+        for t in (2, 3):
+            sent(far_out.at[spot(t)], far_ssem.at[spot(t)])
+        sent(near_out, near_ssem)
 
     @pl.loop(0, 4)
     def _(s):
-        copy(q_send.at[s], q_recv.at[s], q_ssem.at[s], q_rsem.at[s], partner).wait_send()
+        sent(q_send.at[s], q_ssem.at[s])
 
 
 def solution(mesh):
@@ -548,15 +558,17 @@
 
     def per_device(image_embeds, text_embeds):
         out = jax.ShapeDtypeStruct(block, BF16)
-        vmem = pl.BlockSpec(memory_space=pltpu.VMEM)
+        anywhere = pl.BlockSpec(memory_space=pl.ANY)
         return pl.pallas_call(
             lambda *refs: kernel(blocks, *refs),
             out_shape=(out, out),
-            in_specs=[pl.BlockSpec(memory_space=pl.ANY)] * 2,
-            out_specs=(vmem, vmem),
+            in_specs=[anywhere] * 2,
+            out_specs=(anywhere, anywhere),
             scratch_shapes=[
                 pltpu.VMEM(block, BF16),
                 pltpu.VMEM(block, BF16),
+                dma((2,)),
+                pltpu.VMEM((2,) + block, BF16),
                 dma((2,)),
                 pltpu.VMEM((2, 4) + block, BF16),
                 pltpu.VMEM((4,) + block, BF16),
@@ -573,21 +585,22 @@
                 pltpu.VMEM((3,) + block, BF16),
                 pltpu.VMEM((3, THIN, WIDTH), BF16),
                 pltpu.VMEM((3, THIN, WIDTH), BF16),
+                dma((3,)),
                 dma((3, SLICES)),
-                dma((3, SLICES)),
-                dma((4, CHUNKS)),
-                dma((4, CHUNKS)),
-                dma((4, CHUNKS)),
-                dma((2, 4, CHUNKS)),
+                dma((4,)),
                 dma((4,)),
                 dma((4,)),
                 dma((4, CHUNKS)),
-                dma((CHUNKS,)),
+                dma((4,)),
+                dma((4,)),
+                dma((4,)),
+                dma((4,)),
+                dma(()),
                 dma((4, CHUNKS)),
                 dma((4, CHUNKS)),
+                dma((3,)),
                 dma((3, SLICES)),
-                dma((3, SLICES)),
-                dma((2, SLICES)),
+                dma((2,)),
                 dma((3,)),
                 dma((3,)),
                 dma((3,)),

time: 75.4 us -> 72.5 us (0.962)
  Pallas kernels: 71.6 us -> 68.6 us
    pallas_call x1, Pallas kernels: 71.6 us -> 68.6 us  [per_device(): pl.pallas_call(lambda *refs: kernel(blocks, *refs), out_shape=(out, out),...]
where the time goes in v6:
time: 72.5 us; the launch traced here: 71.7 us
  Pallas kernels  68.6 us (95%)
  local copies, waits for them, and re-layouts  2.46 us (3%)
    pallas_call x1, Pallas kernels, per_device(): pl.pallas_call(lambda *refs: kernel(blocks, *refs), out_shape=(out, out),...  68.6 us
    unnamed x4, local copies, waits for them, and re-layouts  2.46 us

profile of v6, /device:TPU:1, one launch (start us, length us, event | category | flops | bytes accessed | tf_op | source)
XLA Modules:
  0.0 71.7 jit_solution(1321750942905857937)
XLA Ops:
  0.6 68.6 %pair_window.1 = (bf16[128,1152]{1,0:T(8,128)(2,1)}, bf16[128,1152]{1,0:T(8,128)(2,1)}) custom-call(bf16[128,1152]{1,0:T(8,128)(2,1)} %refs_0_.1, bf16[128,1152]{1,0:T(8,128)(2,1)} %refs_1_.1), custom_call_target="tpu_custom_call" | custom-call | tf_op jit(solution)/shard_map/pair_window/pallas_call | solution.py:562
  69.3 0.0 copy-start
  69.3 1.7 %copy.6 = bf16[128,1152]{1,0:T(8,128)(2,1)} copy(bf16[128,1152]{1,0:T(8,128)(2,1)} %get-tuple-element.4) | data formatting | bytes 589824
  71.0 0.0 copy-done
  71.0 0.7 copy.7
Async XLA Ops:
  69.3 1.8 %copy-start = (bf16[128,1152]{1,0:T(8,128)(2,1)S(1)}, bf16[128,1152]{1,0:T(8,128)(2,1)}, u32[]{:S(2)}) copy-start(bf16[128,1152]{1,0:T(8,128)(2,1)} %get-tuple-element.5) | copy-start | bytes 884740

commit v7 on v6

--- a/solution.py
+++ b/solution.py
@@ -175,8 +175,16 @@
 
     def text_copy(d, h):
         return copy(
-            txt.at[d, thin(h)], txt.at[d + 1, thin(h)], txt_ssem.at[d], txt_rsem.at[d, h], ahead
+            txt.at[d, thin(h)], txt.at[d + 1, thin(h)], txt_ssem.at[d], txt_rsem.at[d, h // 2], ahead
         )
+
+    def text_arrival(d, g):
+        ref = txt.at[d + 1, rows(g)]
+        copy(ref, ref, txt_ssem.at[d], txt_rsem.at[d, g], ahead).wait_recv()
+
+    def back_arrival(d, g):
+        ref = p_recv.at[d, rows(g)]
+        copy(ref, ref, p_ssem.at[d], p_rsem.at[d, g], behind).wait_recv()
 
     def relay_copy(d, hold, h, ssem):
         return copy(txt.at[d, thin(h)], fwd_hold.at[hold], ssem, fwd_rsem.at[hold], at(0, relay_place(h)))
@@ -196,7 +204,7 @@
 
     def text_relay(d):
         return copy(
-            fwd_hold.at[d], txt.at[d + 1, thin(role)], fwd_ssem.at[d], txt_rsem.at[d, role], next_first
+            fwd_hold.at[d], txt.at[d + 1, thin(role)], fwd_ssem.at[d], txt_rsem.at[d, role // 2], next_first
         )
 
     def text_relay_stage(d):
@@ -210,7 +218,7 @@
         text_start(0, h)
 
     def back_copy(d, h):
-        return copy(p_send.at[d, thin(h)], p_recv.at[d, thin(h)], p_ssem.at[d], p_rsem.at[d, h], behind)
+        return copy(p_send.at[d, thin(h)], p_recv.at[d, thin(h)], p_ssem.at[d], p_rsem.at[d, h // 2], behind)
 
     def back_start(d, h):
         @pl.when(first)
@@ -225,7 +233,7 @@
 
     def back_relay(d):
         return copy(
-            back_hold.at[d], p_recv.at[d, thin(role)], back_ssem.at[d], p_rsem.at[d, role], prev_last
+            back_hold.at[d], p_recv.at[d, thin(role)], back_ssem.at[d], p_rsem.at[d, role // 2], prev_last
         )
 
     def back_relay_stage(d):
@@ -290,11 +298,12 @@
             back_start(d - 1, h)
 
     def back_pass(d):
-        for h in range(SLICES):
-            r = thin(h)
-            back_copy(d, h).wait_recv()
+        for g in range(CHUNKS):
+            r = rows(g)
+            back_arrival(d, g)
             p_send[d - 1, r] = (p_sum[d, r] + p_recv[d, r].astype(F32)).astype(BF16)
-            back_start(d - 1, h)
+            back_start(d - 1, 2 * g)
+            back_start(d - 1, 2 * g + 1)
 
     def image_first(h):
         @pl.when(edge)
@@ -328,7 +337,8 @@
 
     def text_stage(u):
         for h in range(SLICES):
-            text_copy(u, h).wait_recv()
+            if h % 2 == 0:
+                text_arrival(u, h // 2)
             if u == 0:
                 when(ante & (j >= 5), lambda h=h: ante_copy(1, h).start())
                 when(jnp.logical_not(ante & (j >= 5)), text_start, 1, h)
@@ -404,11 +414,14 @@
     late = j >= 5
     soon = j < 5
 
+    favoured = relay & final
     for h in range(CHUNKS // 2):
-        image_first(h)
+        when(jnp.logical_not(favoured), image_first, h)
     when(relay & not_final & not_early, pl.semaphore_wait, fwd_ready, 1)
     when(relay & not_early, text_relay_stage, 0)
     when(relay & not_early, text_relay_stage, 1)
+    for h in range(CHUNKS // 2):
+        when(favoured, image_first, h)
     for h in range(CHUNKS // 2, CHUNKS):
         image_first(h)
     p_sum[...] = jnp.zeros_like(p_sum)
@@ -418,6 +431,9 @@
     when(relay & early, text_relay_stage, 1)
     when(middle, image_stage, 1)
     when(middle & first, image_stage, 2)
+    tardy_first, tardy_second = early & first, early & (place == 1)
+    when(edge & tardy_first, image_stage, 1)
+    when(edge & tardy_first, image_stage, 2)
     text_stage(0)
 
     when(relay & late, text_relay_stage, 2)
@@ -426,7 +442,8 @@
     def _(i):
         recent(jnp.where(i < 2, 1 - i, 2))
 
-    when(edge, image_stage, 1)
+    when(edge & jnp.logical_not(tardy_first), image_stage, 1)
+    when(edge & tardy_second, image_stage, 2)
     when(middle & jnp.logical_not(first), image_stage, 2)
     text_stage(1)
     when(edge, recent, 2)
@@ -435,14 +452,13 @@
     def _(i):
         older(2 - i)
 
-    when(edge, image_stage, 2)
+    when(edge & jnp.logical_not(tardy_first | tardy_second), image_stage, 2)
 
     @pl.when(late & edge)
     def _():
         text_stage(2)
         oldest(1, 3)
 
-    when(edge, far_start, 2)
     recent(3)
     older(3)
 
@@ -457,6 +473,8 @@
 
     when(first, pl.semaphore_wait, lane_ready, SLICES)
     slow = last | (late & (place == 30))
+    hold = relay & (z == 3)
+
     def relay_step(n, here):
         when(relay & late & here, back_relay_stage, 2 - n)
         if n < 2:
@@ -466,19 +484,21 @@
     when(soon, back_begin, 2)
     relay_step(0, not_early)
     when(edge, far_start, 3)
+    when(edge & jnp.logical_not(hold & late), far_start, 2)
     when(late & jnp.logical_not(last), back_pass, 2)
-    when(middle, far_pass, 2)
+    when(middle, far_pass, 3)
     when(relay & early, pl.semaphore_wait, back_ready, 1)
     relay_step(0, early)
-    hold = relay & (z == 3)
     when(edge & jnp.logical_not(hold), far_start, 1)
     when(jnp.logical_not(slow), back_pass, 1)
     relay_step(1, not_early)
-    when(middle, far_pass, 3)
+    when(hold & late, far_start, 2)
+    relay_step(2, not_early)
+    when(middle, near_pass)
     relay_step(1, early)
+    relay_step(2, early)
     when(hold, far_start, 1)
-    relay_step(2, True)
-    when(middle, near_pass)
+    when(middle, far_pass, 2)
     when(late & last, back_pass, 2)
     when(slow, back_pass, 1)
     when(edge, sum_arrival, 0)
@@ -494,8 +514,7 @@
         return pltpu.make_async_copy(out_held.at[which, r], (image_out, text_out)[which].at[r], out_sem.at[which])
 
     for h in range(CHUNKS):
-        for i in range(SLICES // CHUNKS):
-            back_copy(0, SLICES // CHUNKS * h + i).wait_recv()
+        back_arrival(0, h)
         finish(1, h, p_sum[0, rows(h)] + p_recv[0, rows(h)].astype(F32))
 
     for h in range(CHUNKS):
@@ -586,7 +605,7 @@
                 pltpu.VMEM((3, THIN, WIDTH), BF16),
                 pltpu.VMEM((3, THIN, WIDTH), BF16),
                 dma((3,)),
-                dma((3, SLICES)),
+                dma((3, CHUNKS)),
                 dma((4,)),
                 dma((4,)),
                 dma((4,)),
@@ -599,7 +618,7 @@
                 dma((4, CHUNKS)),
                 dma((4, CHUNKS)),
                 dma((3,)),
-                dma((3, SLICES)),
+                dma((3, CHUNKS)),
                 dma((2,)),
                 dma((3,)),
                 dma((3,)),

time: 72.5 us -> 72 us (level)
  the two profiles are of different devices: /device:TPU:1 before, /device:TPU:255 now
where the time goes in v7:
time: 72 us; the launch traced here: 71.9 us
  Pallas kernels  68.8 us (96%)
  local copies, waits for them, and re-layouts  2.46 us (3%)
    pallas_call x1, Pallas kernels, per_device(): pl.pallas_call(lambda *refs: kernel(blocks, *refs), out_shape=(out, out),...  68.8 us
    unnamed x4, local copies, waits for them, and re-layouts  2.46 us

profile of v7, /device:TPU:255, one launch (start us, length us, event | category | flops | bytes accessed | tf_op | source)
XLA Modules:
  0.0 71.9 jit_solution(9221176392761213691)
XLA Ops:
  0.6 68.8 %pair_window.1 = (bf16[128,1152]{1,0:T(8,128)(2,1)}, bf16[128,1152]{1,0:T(8,128)(2,1)}) custom-call(bf16[128,1152]{1,0:T(8,128)(2,1)} %refs_0_.1, bf16[128,1152]{1,0:T(8,128)(2,1)} %refs_1_.1), custom_call_target="tpu_custom_call" | custom-call | tf_op jit(solution)/shard_map/pair_window/pallas_call | solution.py:581
  69.4 0.0 copy-start
  69.4 1.7 %copy.6 = bf16[128,1152]{1,0:T(8,128)(2,1)} copy(bf16[128,1152]{1,0:T(8,128)(2,1)} %get-tuple-element.4) | data formatting | bytes 589824
  71.1 0.0 copy-done
  71.1 0.7 copy.7
Async XLA Ops:
  69.4 1.8 %copy-start = (bf16[128,1152]{1,0:T(8,128)(2,1)S(1)}, bf16[128,1152]{1,0:T(8,128)(2,1)}, u32[]{:S(2)}) copy-start(bf16[128,1152]{1,0:T(8,128)(2,1)} %get-tuple-element.5) | copy-start | bytes 884740

commit v8 on v7

--- a/solution.py
+++ b/solution.py
@@ -492,8 +492,8 @@
     when(edge & jnp.logical_not(hold), far_start, 1)
     when(jnp.logical_not(slow), back_pass, 1)
     relay_step(1, not_early)
+    relay_step(2, not_early)
     when(hold & late, far_start, 2)
-    relay_step(2, not_early)
     when(middle, near_pass)
     relay_step(1, early)
     relay_step(2, early)

time: 72 us -> 70.9 us (0.985)
  the two profiles are of different devices: /device:TPU:255 before, /device:TPU:137 now
where the time goes in v8:
time: 70.9 us; the launch traced here: 70.7 us
  Pallas kernels  67.6 us (95%)
  local copies, waits for them, and re-layouts  2.46 us (3%)
    pallas_call x1, Pallas kernels, per_device(): pl.pallas_call(lambda *refs: kernel(blocks, *refs), out_shape=(out, out),...  67.6 us
    unnamed x4, local copies, waits for them, and re-layouts  2.46 us

profile of v8, /device:TPU:137, one launch (start us, length us, event | category | flops | bytes accessed | tf_op | source)
XLA Modules:
  0.0 70.7 jit_solution(930551961955277452)
XLA Ops:
  0.6 67.6 %pair_window.1 = (bf16[128,1152]{1,0:T(8,128)(2,1)}, bf16[128,1152]{1,0:T(8,128)(2,1)}) custom-call(bf16[128,1152]{1,0:T(8,128)(2,1)} %refs_0_.1, bf16[128,1152]{1,0:T(8,128)(2,1)} %refs_1_.1), custom_call_target="tpu_custom_call" | custom-call | tf_op jit(solution)/shard_map/pair_window/pallas_call | solution.py:581
  68.3 0.0 copy-start
  68.3 1.7 %copy.6 = bf16[128,1152]{1,0:T(8,128)(2,1)} copy(bf16[128,1152]{1,0:T(8,128)(2,1)} %get-tuple-element.4) | data formatting | bytes 589824
  70.0 0.0 copy-done
  70.0 0.7 %copy.7 = bf16[128,1152]{1,0:T(8,128)(2,1)} copy(bf16[128,1152]{1,0:T(8,128)(2,1)S(1)} %copy-done) | data formatting | bytes 589824
Async XLA Ops:
  68.3 1.8 %copy-start = (bf16[128,1152]{1,0:T(8,128)(2,1)S(1)}, bf16[128,1152]{1,0:T(8,128)(2,1)}, u32[]{:S(2)}) copy-start(bf16[128,1152]{1,0:T(8,128)(2,1)} %get-tuple-element.5) | copy-start | bytes 884740
